TPU v7x, 512 devices: a whole 4x8x8 slice. The times are simulated.
512 devices in a mesh: gx: 8 (over y), gy: 8 (over z), gz: 8 (over x, core).
Axes of the slice: x: 4, y: 8, z: 8, core: 2. Of those that a mesh axis runs over, the one named last changes fastest.
Arguments:
- source: float32 [2, 32, 64, 1024], P(None, 'gx', 'gy', 'gz'), may hold values from -6 to 6
- sigma_intra: float32 [3, 32, 64, 1024], P(None, 'gx', 'gy', 'gz'), may hold values from 0.3 to 3
- sigma_extra: float32 [3, 32, 64, 1024], P(None, 'gx', 'gy', 'gz'), may hold values from 0.5 to 3
- membrane: float32 [32, 64, 1024], P('gx', 'gy', 'gz'), may hold values from 0.5 to 5
Outputs:
- solution: float32 [2, 32, 64, 1024], P(None, 'gx', 'gy', 'gz')
- residual: float32 [2, 32, 64, 1024], P(None, 'gx', 'gy', 'gz')
All inputs are finite; a program needn't handle non-finite values.
Results may differ from a plain program's by a relative error of at most 0.0009.
Values sent between devices are 32-bit elements; how exact they have to be, the bound alone decides.
A program may use at most 64 MiB of HBM per device.

v0:
```python
import jax
import jax.numpy as jnp
from jax import lax
from jax.sharding import Mesh
from jax.sharding import PartitionSpec as P

KRYLOV = 10
GZ = ("gz_0", "gz_1")


highest = lax.Precision.HIGHEST


def with_halo(x, sides, width):
    edges = {}
    for axis, dim in sides:
        size, length = (lax.axis_size(axis), x.shape[dim])
        up = [(i, (i + 1) % size) for i in range(size - 1)]
        last = lax.slice_in_dim(x, length - width, length, axis=dim)
        initial = lax.slice_in_dim(x, 0, width, axis=dim)
        edges[dim] = (
            lax.ppermute(last, axis, up),
            lax.ppermute(initial, axis, [(b, a) for a, b in up]),
        )
    done = []
    for _, dim in sides:
        low, high = edges[dim]
        around = [(width, width) if d in done else (0, 0) for d in range(x.ndim)]
        x = jnp.concatenate([jnp.pad(low, around), x, jnp.pad(high, around)], axis=dim)
        done.append(dim)
    return x


def copy_for_each(x, axis):
    copies = jnp.broadcast_to(x, (lax.axis_size(axis), *x.shape))
    return lax.all_to_all(copies, axis, split_axis=0, concat_axis=0, tiled=True)


def of_everyone(x, axis):
    return copy_for_each(x, axis).sum(axis=0)


def by_axis(x, axes):
    far, near = axes
    return of_everyone(of_everyone(x, near), far)


def packed_total(arrays, axis):
    ravelled, at, done = (jnp.concatenate([a.reshape(-1) for a in arrays]), 0, [])
    so_far = by_axis(ravelled, axis)
    for a in arrays:
        done.append(so_far[at : at + a.size].reshape(a.shape))
        at += a.size
    return tuple(done)


def shifted(padded_grid, spatial, offset):
    pieces = [slice(1, -1), slice(1, -1), slice(1, -1)]
    if offset > 0:
        pieces[spatial] = slice(2, None)
    else:
        pieces[spatial] = slice(None, -2)
    return padded_grid[tuple(pieces)]


def face_terms(padded_sigma):
    upper_faces = []
    lower_faces = []
    for spatial in range(3):
        component = padded_sigma[spatial]
        middle = component[1:-1, 1:-1, 1:-1]
        upper_faces.append(0.5 * (middle + shifted(component, spatial, 1)))
        lower_faces.append(0.5 * (middle + shifted(component, spatial, -1)))
    diagonal = upper_faces[0] + lower_faces[0]
    for spatial in range(1, 3):
        diagonal = diagonal + upper_faces[spatial] + lower_faces[spatial]
    return (upper_faces, lower_faces, diagonal)


def apply_laplace(faces, padded_field):
    upper_faces, lower_faces, diagonal = faces
    result = diagonal * padded_field[1:-1, 1:-1, 1:-1]
    for spatial in range(3):
        result = result - upper_faces[spatial] * shifted(padded_field, spatial, 1)
        result = result - lower_faces[spatial] * shifted(padded_field, spatial, -1)
    return result


def operate(intra_faces, extra_faces, membrane, padded_pair):
    joined = padded_pair[0] + padded_pair[1]
    shared = apply_laplace(intra_faces, joined)
    leading = membrane * padded_pair[0, 1:-1, 1:-1, 1:-1] + shared
    second = shared + apply_laplace(extra_faces, padded_pair[1])
    return jnp.stack([leading, second])


def inverse_blocks(intra_faces, extra_faces, membrane):
    intra_sum = intra_faces[2]
    extra_sum = extra_faces[2]
    determinant = membrane * intra_sum + membrane * extra_sum + intra_sum * extra_sum
    return jnp.stack(
        [
            (intra_sum + extra_sum) / determinant,
            -intra_sum / determinant,
            (membrane + intra_sum) / determinant,
        ]
    )


def precondition(inverse, pair):
    leading = inverse[0] * pair[0] + inverse[1] * pair[1]
    second = inverse[1] * pair[0] + inverse[2] * pair[1]
    return jnp.stack([leading, second])


def least_squares(hessenberg, start_norm):
    krylov = hessenberg.shape[1]
    rotated = hessenberg
    target = jnp.zeros((krylov + 1,), jnp.float32).at[0].set(start_norm)
    for column in range(krylov):
        pivot = rotated[column, column]
        lower_entry = rotated[column + 1, column]
        radius = jnp.sqrt(pivot * pivot + lower_entry * lower_entry)
        cosine = pivot / radius
        sine_value = lower_entry / radius
        row_top = cosine * rotated[column] + sine_value * rotated[column + 1]
        row_below = -sine_value * rotated[column] + cosine * rotated[column + 1]
        rotated = rotated.at[column].set(row_top).at[column + 1].set(row_below)
        leading = cosine * target[column] + sine_value * target[column + 1]
        second = -sine_value * target[column] + cosine * target[column + 1]
        target = target.at[column].set(leading).at[column + 1].set(second)
    coeffs = jnp.zeros((krylov,), jnp.float32)
    for column in range(krylov - 1, -1, -1):
        partial_sum = jnp.sum(rotated[column, column + 1 :] * coeffs[column + 1 :])
        coeffs = coeffs.at[column].set((target[column] - partial_sum) / rotated[column, column])
    return coeffs


def body(source, sigma_intra, sigma_extra, membrane):
    stacked = jnp.concatenate([sigma_intra, sigma_extra], 0)
    padded_sigma = with_halo(stacked, (("gx", 1), ("gy", 2), (GZ, 3)), 1)
    intra_faces = face_terms(padded_sigma[:3])
    extra_faces = face_terms(padded_sigma[3:])
    inverse = inverse_blocks(intra_faces, extra_faces, membrane)
    padded_inverse = with_halo(inverse, (("gx", 1), ("gy", 2), (GZ, 3)), 1)
    start_norm = jnp.sqrt(by_axis(jnp.sum(source * source), (("gx", "gy"), ("gz_0", "gz_1"))))
    basis = jnp.zeros((KRYLOV + 1,) + source.shape, jnp.float32).at[0].set(source / start_norm)
    hessenberg = jnp.zeros((KRYLOV + 1, KRYLOV), jnp.float32)
    for column in range(KRYLOV):
        padded_vector = with_halo(basis[column], (("gx", 1), ("gy", 2), (GZ, 3)), 1)
        padded_solved = precondition(padded_inverse, padded_vector)
        applied = operate(intra_faces, extra_faces, membrane, padded_solved)
        flat_basis = basis[: column + 1].reshape(column + 1, -1)
        local_project = jnp.dot(flat_basis, applied.reshape(-1), precision=highest)
        project, total = packed_total(
            (local_project, jnp.sum(applied * applied)), (("gx", "gy"), ("gz_0", "gz_1"))
        )
        applied = applied - jnp.dot(project, flat_basis, precision=highest).reshape(applied.shape)
        norm_sq = total - jnp.sum(project * project)
        new_norm = jnp.sqrt(norm_sq)
        basis = basis.at[column + 1].set(applied / new_norm)
        hessenberg = (
            hessenberg.at[: column + 1, column].set(project).at[column + 1, column].set(new_norm)
        )
    coeffs = least_squares(hessenberg, start_norm)
    combined = jnp.dot(coeffs, basis[:KRYLOV].reshape(KRYLOV, -1), precision=highest).reshape(
        source.shape
    )
    solution = precondition(inverse, combined)
    remainder = jnp.zeros((KRYLOV + 1,), jnp.float32).at[0].set(start_norm) - jnp.dot(
        hessenberg, coeffs, precision=highest
    )
    residual = jnp.dot(remainder, basis.reshape(KRYLOV + 1, -1), precision=highest).reshape(
        source.shape
    )
    return (solution, residual)


def solution(mesh):
    torus = Mesh(
        mesh.devices.reshape(mesh.shape["gx"], mesh.shape["gy"], 4, 2), ("gx", "gy", "gz_0", "gz_1")
    )
    return jax.shard_map(
        body,
        mesh=torus,
        in_specs=(
            P(None, "gx", "gy", GZ),
            P(None, "gx", "gy", GZ),
            P(None, "gx", "gy", GZ),
            P("gx", "gy", GZ),
        ),
        out_specs=(P(None, "gx", "gy", GZ), P(None, "gx", "gy", GZ)),
        check_vma=False,
    )
```

profile of v0, /device:TPU:1, one launch (start us, length us, event | category | flops | bytes accessed | tf_op | source)
XLA Modules:
  0.0 710.9 jit_solution(4066487713449410849)
XLA Ops:
  1.6 4.5 collective-permute-start
  6.1 5.5 collective-permute-start.5
  18.4 5.6 all-to-all-start
  30.7 17.8 %all-to-all-start.1 = ((f32[64,1,1]{2,1,0:T(1,128)}), f32[64,1,1]{2,1,0:T(1,128)S(1)}, u32[]{:S(2)}, u32[]{:S(2)}) async-start(f32[64,1,1]{2,1,0:T(1,128)} %broadcast_in_dim.69), calls=%async_computation.1 | async-start | bytes 65536 | tf_op jit(solution)/shard_map/all_to_all | solution.py:36
  49.3 10.1 %all-to-all-done.1 = f32[64,1,1]{2,1,0:T(1,128)S(1)} async-done(((f32[64,1,1]{2,1,0:T(1,128)}), f32[64,1,1]{2,1,0:T(1,128)S(1)}, u32[]{:S(2)}, u32[]{:S(2)}) %all-to-all-start.1) | async-done | bytes 288 | tf_op jit(solution)/shard_map/all_to_all | solution.py:36
  62.1 4.9 collective-permute-start.12
  72.6 4.3 collective-permute-start.13
  82.9 4.6 collective-permute-start.7
  87.5 4.8 collective-permute-start.6
  92.3 4.3 collective-permute-start.8
  104.1 4.8 all-to-all-start.2
  114.1 9.1 %all-to-all-start.3 = ((f32[64,1,2]{2,1,0:T(1,128)}), f32[64,1,2]{2,1,0:T(1,128)S(1)}, u32[]{:S(2)}, u32[]{:S(2)}) async-start(f32[64,1,2]{2,1,0:T(1,128)} %broadcast_in_dim.71), calls=%async_computation.3 | async-start | bytes 65536 | tf_op jit(solution)/shard_map/all_to_all | solution.py:36
  123.3 10.7 %all-to-all-done.3 = f32[64,1,2]{2,1,0:T(1,128)S(1)} async-done(((f32[64,1,2]{2,1,0:T(1,128)}), f32[64,1,2]{2,1,0:T(1,128)S(1)}, u32[]{:S(2)}, u32[]{:S(2)}) %all-to-all-start.3) | async-done | bytes 544 | tf_op jit(solution)/shard_map/all_to_all | solution.py:36
  137.4 4.2 collective-permute-start.18
  156.7 5.7 all-to-all-start.4
  167.6 7.2 %all-to-all-start.5 = ((f32[64,1,3]{2,1,0:T(1,128)}), f32[64,1,3]{2,1,0:T(1,128)S(1)}, u32[]{:S(2)}, u32[]{:S(2)}) async-start(f32[64,1,3]{2,1,0:T(1,128)} %broadcast_in_dim.73), calls=%async_computation.5 | async-start | bytes 65536 | tf_op jit(solution)/shard_map/all_to_all | solution.py:36
  175.0 10.7 %all-to-all-done.5 = f32[64,1,3]{2,1,0:T(1,128)S(1)} async-done(((f32[64,1,3]{2,1,0:T(1,128)}), f32[64,1,3]{2,1,0:T(1,128)S(1)}, u32[]{:S(2)}, u32[]{:S(2)}) %all-to-all-start.5) | async-done | bytes 800 | tf_op jit(solution)/shard_map/all_to_all | solution.py:36
  188.8 4.2 collective-permute-start.24
  208.1 5.7 all-to-all-start.6
  213.9 4.5 all-to-all-done.6
  219.0 7.2 %all-to-all-start.7 = ((f32[64,1,4]{2,1,0:T(1,128)}), f32[64,1,4]{2,1,0:T(1,128)S(1)}, u32[]{:S(2)}, u32[]{:S(2)}) async-start(f32[64,1,4]{2,1,0:T(1,128)} %broadcast_in_dim.75), calls=%async_computation.7 | async-start | bytes 65536 | tf_op jit(solution)/shard_map/all_to_all | solution.py:36
  227.0 10.1 %all-to-all-done.7 = f32[64,1,4]{2,1,0:T(1,128)S(1)} async-done(((f32[64,1,4]{2,1,0:T(1,128)}), f32[64,1,4]{2,1,0:T(1,128)S(1)}, u32[]{:S(2)}, u32[]{:S(2)}) %all-to-all-start.7) | async-done | bytes 1056 | tf_op jit(solution)/shard_map/all_to_all | solution.py:36
  240.2 4.2 collective-permute-start.30
  259.6 5.7 all-to-all-start.8
  270.5 7.2 %all-to-all-start.9 = ((f32[64,1,5]{2,1,0:T(1,128)}), f32[64,1,5]{2,1,0:T(1,128)S(1)}, u32[]{:S(2)}, u32[]{:S(2)}) async-start(f32[64,1,5]{2,1,0:T(1,128)} %broadcast_in_dim.77), calls=%async_computation.9 | async-start | bytes 65536 | tf_op jit(solution)/shard_map/all_to_all | solution.py:36
  277.8 10.7 %all-to-all-done.9 = f32[64,1,5]{2,1,0:T(1,128)S(1)} async-done(((f32[64,1,5]{2,1,0:T(1,128)}), f32[64,1,5]{2,1,0:T(1,128)S(1)}, u32[]{:S(2)}, u32[]{:S(2)}) %all-to-all-start.9) | async-done | bytes 1312 | tf_op jit(solution)/shard_map/all_to_all | solution.py:36
  291.6 4.2 collective-permute-start.36
  311.0 5.7 all-to-all-start.10
  316.7 4.5 all-to-all-done.10
  321.9 7.2 %all-to-all-start.11 = ((f32[64,1,6]{2,1,0:T(1,128)}), f32[64,1,6]{2,1,0:T(1,128)S(1)}, u32[]{:S(2)}, u32[]{:S(2)}) async-start(f32[64,1,6]{2,1,0:T(1,128)} %broadcast_in_dim.79), calls=%async_computation.11 | async-start | bytes 65536 | tf_op jit(solution)/shard_map/all_to_all | solution.py:36
  329.9 10.0 %all-to-all-done.11 = f32[64,1,6]{2,1,0:T(1,128)S(1)} async-done(((f32[64,1,6]{2,1,0:T(1,128)}), f32[64,1,6]{2,1,0:T(1,128)S(1)}, u32[]{:S(2)}, u32[]{:S(2)}) %all-to-all-start.11) | async-done | bytes 1568 | tf_op jit(solution)/shard_map/all_to_all | solution.py:36
  342.9 4.2 collective-permute-start.42
  362.3 5.7 all-to-all-start.12
  373.2 7.2 %all-to-all-start.13 = ((f32[64,1,7]{2,1,0:T(1,128)}), f32[64,1,7]{2,1,0:T(1,128)S(1)}, u32[]{:S(2)}, u32[]{:S(2)}) async-start(f32[64,1,7]{2,1,0:T(1,128)} %broadcast_in_dim.81), calls=%async_computation.13 | async-start | bytes 65536 | tf_op jit(solution)/shard_map/all_to_all | solution.py:36
  380.6 10.7 %all-to-all-done.13 = f32[64,1,7]{2,1,0:T(1,128)S(1)} async-done(((f32[64,1,7]{2,1,0:T(1,128)}), f32[64,1,7]{2,1,0:T(1,128)S(1)}, u32[]{:S(2)}, u32[]{:S(2)}) %all-to-all-start.13) | async-done | bytes 1824 | tf_op jit(solution)/shard_map/all_to_all | solution.py:36
  394.4 4.2 collective-permute-start.48
  418.9 4.4 all-to-all-done.14
  424.0 8.8 %all-to-all-start.15 = ((f32[64,1,8]{2,1,0:T(1,128)}), f32[64,1,8]{2,1,0:T(1,128)S(1)}, u32[]{:S(2)}, u32[]{:S(2)}) async-start(f32[64,1,8]{2,1,0:T(1,128)} %broadcast_in_dim.83), calls=%async_computation.15 | async-start | bytes 65536 | tf_op jit(solution)/shard_map/all_to_all | solution.py:36
  436.5 7.1 all-to-all-done.15
  446.6 4.4 collective-permute-start.54
  478.4 10.2 %all-to-all-start.17 = ((f32[64,1,9]{2,1,0:T(1,128)}), f32[64,1,9]{2,1,0:T(1,128)S(1)}, u32[]{:S(2)}, u32[]{:S(2)}) async-start(f32[64,1,9]{2,1,0:T(1,128)} %broadcast_in_dim.85), calls=%async_computation.17 | async-start | bytes 65536 | tf_op jit(solution)/shard_map/all_to_all | solution.py:36
  492.2 7.1 all-to-all-done.17
  502.4 4.2 collective-permute-start.60
  534.5 10.1 %all-to-all-start.19 = ((f32[64,1,10]{2,1,0:T(1,128)}), f32[64,1,10]{2,1,0:T(1,128)S(1)}, u32[]{:S(2)}, u32[]{:S(2)}) async-start(f32[64,1,10]{2,1,0:T(1,128)} %broadcast_in_dim.87), calls=%async_computation.19 | async-start | bytes 65536 | tf_op jit(solution)/shard_map/all_to_all | solution.py:36
  544.6 10.8 %all-to-all-done.19 = f32[64,1,10]{2,1,0:T(1,128)S(1)} async-done(((f32[64,1,10]{2,1,0:T(1,128)}), f32[64,1,10]{2,1,0:T(1,128)S(1)}, u32[]{:S(2)}, u32[]{:S(2)}) %all-to-all-start.19) | async-done | bytes 2592 | tf_op jit(solution)/shard_map/all_to_all | solution.py:36
  585.8 4.5 all-to-all-done.20
  591.0 8.8 %all-to-all-start.21 = ((f32[64,1,11]{2,1,0:T(1,128)}), f32[64,1,11]{2,1,0:T(1,128)S(1)}, u32[]{:S(2)}, u32[]{:S(2)}) async-start(f32[64,1,11]{2,1,0:T(1,128)} %broadcast_in_dim.89), calls=%async_computation.21 | async-start | bytes 65536 | tf_op jit(solution)/shard_map/all_to_all | solution.py:36
  603.4 7.1 all-to-all-done.21
  (533 shorter events, 298.3 us)
Async XLA Ops:
  1.6 59.2 %collective-permute-start = (f32[6,4,8,1]{3,2,1,0:T(8,128)S(1)}, f32[6,4,8,1]{3,2,1,0:T(8,128)S(1)}, u32[]{:S(2)}, u32[]{:S(2)}) collective-permute-start(f32[6,4,8,1]{3,2,1,0:T(8,128)S(1)} %get-tuple-element.1087), channel_id=1, source_target_pairs={{0,1},{1,2},{2,3},{3,4},{4,5},{5,6},{6,7},{8,9},{9,10},{10,11},{11... | collective-permute-start | bytes 2312 | tf_op jit(solution)/shard_map/ppermute | solution.py:22
  6.1 56.1 %collective-permute-start.5 = (f32[6,4,8,1]{3,2,1,0:T(8,128)S(1)}, f32[6,4,8,1]{3,2,1,0:T(8,128)S(1)}, u32[]{:S(2)}, u32[]{:S(2)}) collective-permute-start(f32[6,4,8,1]{3,2,1,0:T(8,128)S(1)} %get-tuple-element.1088), channel_id=1, source_target_pairs={{1,0},{2,1},{3,2},{4,3},{5,4},{6,5},{7,6},{9,8},{10,9},{11,10},{12... | collective-permute-start | bytes 2312 | tf_op jit(solution)/shard_map/ppermute | solution.py:23
  11.6 59.7 %collective-permute-start.2 = (f32[6,1,8,128]{3,2,1,0:T(8,128)S(1)}, f32[6,1,8,128]{3,2,1,0:T(8,128)S(1)}, u32[]{:S(2)}, u32[]{:S(2)}) collective-permute-start(f32[6,1,8,128]{3,2,1,0:T(8,128)S(1)} %get-tuple-element.1085), channel_id=1, source_target_pairs={{0,64},{64,128},{128,192},{192,256},{256,320},{320,384},{384,448},... | collective-permute-start | bytes 73736 | tf_op jit(solution)/shard_map/ppermute | solution.py:22
  12.9 59.7 %collective-permute-start.3 = (f32[6,1,8,128]{3,2,1,0:T(8,128)S(1)}, f32[6,1,8,128]{3,2,1,0:T(8,128)S(1)}, u32[]{:S(2)}, u32[]{:S(2)}) collective-permute-start(f32[6,1,8,128]{3,2,1,0:T(8,128)S(1)} %get-tuple-element.1086), channel_id=1, source_target_pairs={{64,0},{128,64},{192,128},{256,192},{320,256},{384,320},{448,384},... | collective-permute-start | bytes 73736 | tf_op jit(solution)/shard_map/ppermute | solution.py:23
  14.3 52.8 %collective-permute-start.1 = (f32[6,4,1,128]{3,2,1,0:T(1,128)S(1)}, f32[6,4,1,128]{3,2,1,0:T(1,128)S(1)}, u32[]{:S(2)}, u32[]{:S(2)}) collective-permute-start(f32[6,4,1,128]{3,2,1,0:T(1,128)S(1)} %get-tuple-element.1089), channel_id=1, source_target_pairs={{0,8},{8,16},{16,24},{24,32},{32,40},{40,48},{48,56},{1,9},{9,17},... | collective-permute-start | bytes 36872 | tf_op jit(solution)/shard_map/ppermute | solution.py:22
  18.4 10.4 %all-to-all-start = ((f32[8,1,1]{2,1,0:T(1,128)}), f32[8,1,1]{2,1,0:T(1,128)S(1)}, u32[]{:S(2)}, u32[]{:S(2)}) async-start(f32[8,1,1]{2,1,0:T(1,128)} %broadcast_in_dim.68), calls=%async_computation | async-start | bytes 8192 | tf_op jit(solution)/shard_map/all_to_all | solution.py:36
  30.7 28.6 %all-to-all-start.1 = ((f32[64,1,1]{2,1,0:T(1,128)}), f32[64,1,1]{2,1,0:T(1,128)S(1)}, u32[]{:S(2)}, u32[]{:S(2)}) async-start(f32[64,1,1]{2,1,0:T(1,128)} %broadcast_in_dim.69), calls=%async_computation.1 | async-start | bytes 65536 | tf_op jit(solution)/shard_map/all_to_all | solution.py:36
  62.1 16.1 %collective-permute-start.12 = (f32[2,4,8,1]{3,2,1,0:T(8,128)S(1)}, f32[2,4,8,1]{3,2,1,0:T(8,128)S(1)}, u32[]{:S(2)}, u32[]{:S(2)}) collective-permute-start(f32[2,4,8,1]{3,2,1,0:T(8,128)S(1)} %get-tuple-element.1173), channel_id=1, source_target_pairs={{0,1},{1,2},{2,3},{3,4},{4,5},{5,6},{6,7},{8,9},{9,10},{10,11},{11... | collective-permute-start | bytes 776 | tf_op jit(solution)/shard_map/ppermute | solution.py:22
  67.1 12.5 %collective-permute-start.17 = (f32[2,4,8,1]{3,2,1,0:T(8,128)S(1)}, f32[2,4,8,1]{3,2,1,0:T(8,128)S(1)}, u32[]{:S(2)}, u32[]{:S(2)}) collective-permute-start(f32[2,4,8,1]{3,2,1,0:T(8,128)S(1)} %get-tuple-element.1174), channel_id=1, source_target_pairs={{1,0},{2,1},{3,2},{4,3},{5,4},{6,5},{7,6},{9,8},{10,9},{11,10},{12... | collective-permute-start | bytes 776 | tf_op jit(solution)/shard_map/ppermute | solution.py:23
  69.0 18.5 %collective-permute-start.14 = (f32[2,1,8,128]{3,2,1,0:T(8,128)S(1)}, f32[2,1,8,128]{3,2,1,0:T(8,128)S(1)}, u32[]{:S(2)}, u32[]{:S(2)}) collective-permute-start(f32[2,1,8,128]{3,2,1,0:T(8,128)S(1)} %get-tuple-element.1171), channel_id=1, source_target_pairs={{0,64},{64,128},{128,192},{192,256},{256,320},{320,384},{384,448},... | collective-permute-start | bytes 24584 | tf_op jit(solution)/shard_map/ppermute | solution.py:22
  71.3 21.0 %collective-permute-start.15 = (f32[2,1,8,128]{3,2,1,0:T(8,128)S(1)}, f32[2,1,8,128]{3,2,1,0:T(8,128)S(1)}, u32[]{:S(2)}, u32[]{:S(2)}) collective-permute-start(f32[2,1,8,128]{3,2,1,0:T(8,128)S(1)} %get-tuple-element.1172), channel_id=1, source_target_pairs={{64,0},{128,64},{192,128},{256,192},{320,256},{384,320},{448,384},... | collective-permute-start | bytes 24584 | tf_op jit(solution)/shard_map/ppermute | solution.py:23
  79.6 18.4 %collective-permute-start.10 = (f32[3,4,1,128]{3,2,1,0:T(1,128)S(1)}, f32[3,4,1,128]{3,2,1,0:T(1,128)S(1)}, u32[]{:S(2)}, u32[]{:S(2)}) collective-permute-start(f32[3,4,1,128]{3,2,1,0:T(1,128)S(1)} %get-tuple-element.1098), channel_id=1, source_target_pairs={{8,0},{16,8},{24,16},{32,24},{40,32},{48,40},{56,48},{9,1},{17,9},... | collective-permute-start | bytes 18440 | tf_op jit(solution)/shard_map/ppermute | solution.py:23
  80.9 15.6 %collective-permute-start.11 = (f32[3,4,8,1]{3,2,1,0:T(8,128)S(1)}, f32[3,4,8,1]{3,2,1,0:T(8,128)S(1)}, u32[]{:S(2)}, u32[]{:S(2)}) collective-permute-start(f32[3,4,8,1]{3,2,1,0:T(8,128)S(1)} %get-tuple-element.1096), channel_id=1, source_target_pairs={{1,0},{2,1},{3,2},{4,3},{5,4},{6,5},{7,6},{9,8},{10,9},{11,10},{12... | collective-permute-start | bytes 1160 | tf_op jit(solution)/shard_map/ppermute | solution.py:23
  82.9 15.2 %collective-permute-start.7 = (f32[3,4,1,128]{3,2,1,0:T(1,128)S(1)}, f32[3,4,1,128]{3,2,1,0:T(1,128)S(1)}, u32[]{:S(2)}, u32[]{:S(2)}) collective-permute-start(f32[3,4,1,128]{3,2,1,0:T(1,128)S(1)} %get-tuple-element.1097), channel_id=1, source_target_pairs={{0,8},{8,16},{16,24},{24,32},{32,40},{40,48},{48,56},{1,9},{9,17},... | collective-permute-start | bytes 18440 | tf_op jit(solution)/shard_map/ppermute | solution.py:22
  87.5 10.5 %collective-permute-start.6 = (f32[3,4,8,1]{3,2,1,0:T(8,128)S(1)}, f32[3,4,8,1]{3,2,1,0:T(8,128)S(1)}, u32[]{:S(2)}, u32[]{:S(2)}) collective-permute-start(f32[3,4,8,1]{3,2,1,0:T(8,128)S(1)} %get-tuple-element.1095), channel_id=1, source_target_pairs={{0,1},{1,2},{2,3},{3,4},{4,5},{5,6},{6,7},{8,9},{9,10},{10,11},{11... | collective-permute-start | bytes 1160 | tf_op jit(solution)/shard_map/ppermute | solution.py:22
  114.1 19.9 %all-to-all-start.3 = ((f32[64,1,2]{2,1,0:T(1,128)}), f32[64,1,2]{2,1,0:T(1,128)S(1)}, u32[]{:S(2)}, u32[]{:S(2)}) async-start(f32[64,1,2]{2,1,0:T(1,128)} %broadcast_in_dim.71), calls=%async_computation.3 | async-start | bytes 65536 | tf_op jit(solution)/shard_map/all_to_all | solution.py:36
  137.4 11.9 %collective-permute-start.18 = (f32[2,4,8,1]{3,2,1,0:T(8,128)S(1)}, f32[2,4,8,1]{3,2,1,0:T(8,128)S(1)}, u32[]{:S(2)}, u32[]{:S(2)}) collective-permute-start(f32[2,4,8,1]{3,2,1,0:T(8,128)S(1)} %get-tuple-element.1167), channel_id=1, source_target_pairs={{0,1},{1,2},{2,3},{3,4},{4,5},{5,6},{6,7},{8,9},{9,10},{10,11},{11... | collective-permute-start | bytes 776 | tf_op jit(solution)/shard_map/ppermute | solution.py:22
  156.7 10.2 %all-to-all-start.4 = ((f32[8,1,3]{2,1,0:T(1,128)}), f32[8,1,3]{2,1,0:T(1,128)S(1)}, u32[]{:S(2)}, u32[]{:S(2)}) async-start(f32[8,1,3]{2,1,0:T(1,128)} %broadcast_in_dim.72), calls=%async_computation.4 | async-start | bytes 8192 | tf_op jit(solution)/shard_map/all_to_all | solution.py:36
  167.6 18.1 %all-to-all-start.5 = ((f32[64,1,3]{2,1,0:T(1,128)}), f32[64,1,3]{2,1,0:T(1,128)S(1)}, u32[]{:S(2)}, u32[]{:S(2)}) async-start(f32[64,1,3]{2,1,0:T(1,128)} %broadcast_in_dim.73), calls=%async_computation.5 | async-start | bytes 65536 | tf_op jit(solution)/shard_map/all_to_all | solution.py:36
  188.8 11.9 %collective-permute-start.24 = (f32[2,4,8,1]{3,2,1,0:T(8,128)S(1)}, f32[2,4,8,1]{3,2,1,0:T(8,128)S(1)}, u32[]{:S(2)}, u32[]{:S(2)}) collective-permute-start(f32[2,4,8,1]{3,2,1,0:T(8,128)S(1)} %get-tuple-element.1159), channel_id=1, source_target_pairs={{0,1},{1,2},{2,3},{3,4},{4,5},{5,6},{6,7},{8,9},{9,10},{10,11},{11... | collective-permute-start | bytes 776 | tf_op jit(solution)/shard_map/ppermute | solution.py:22
  208.1 10.2 %all-to-all-start.6 = ((f32[8,1,4]{2,1,0:T(1,128)}), f32[8,1,4]{2,1,0:T(1,128)S(1)}, u32[]{:S(2)}, u32[]{:S(2)}) async-start(f32[8,1,4]{2,1,0:T(1,128)} %broadcast_in_dim.74), calls=%async_computation.6 | async-start | bytes 8192 | tf_op jit(solution)/shard_map/all_to_all | solution.py:36
  219.0 18.1 %all-to-all-start.7 = ((f32[64,1,4]{2,1,0:T(1,128)}), f32[64,1,4]{2,1,0:T(1,128)S(1)}, u32[]{:S(2)}, u32[]{:S(2)}) async-start(f32[64,1,4]{2,1,0:T(1,128)} %broadcast_in_dim.75), calls=%async_computation.7 | async-start | bytes 65536 | tf_op jit(solution)/shard_map/all_to_all | solution.py:36
  240.2 11.9 %collective-permute-start.30 = (f32[2,4,8,1]{3,2,1,0:T(8,128)S(1)}, f32[2,4,8,1]{3,2,1,0:T(8,128)S(1)}, u32[]{:S(2)}, u32[]{:S(2)}) collective-permute-start(f32[2,4,8,1]{3,2,1,0:T(8,128)S(1)} %get-tuple-element.1151), channel_id=1, source_target_pairs={{0,1},{1,2},{2,3},{3,4},{4,5},{5,6},{6,7},{8,9},{9,10},{10,11},{11... | collective-permute-start | bytes 776 | tf_op jit(solution)/shard_map/ppermute | solution.py:22
  270.5 18.1 %all-to-all-start.9 = ((f32[64,1,5]{2,1,0:T(1,128)}), f32[64,1,5]{2,1,0:T(1,128)S(1)}, u32[]{:S(2)}, u32[]{:S(2)}) async-start(f32[64,1,5]{2,1,0:T(1,128)} %broadcast_in_dim.77), calls=%async_computation.9 | async-start | bytes 65536 | tf_op jit(solution)/shard_map/all_to_all | solution.py:36
  291.6 11.9 %collective-permute-start.36 = (f32[2,4,8,1]{3,2,1,0:T(8,128)S(1)}, f32[2,4,8,1]{3,2,1,0:T(8,128)S(1)}, u32[]{:S(2)}, u32[]{:S(2)}) collective-permute-start(f32[2,4,8,1]{3,2,1,0:T(8,128)S(1)} %get-tuple-element.1143), channel_id=1, source_target_pairs={{0,1},{1,2},{2,3},{3,4},{4,5},{5,6},{6,7},{8,9},{9,10},{10,11},{11... | collective-permute-start | bytes 776 | tf_op jit(solution)/shard_map/ppermute | solution.py:22
  321.9 18.1 %all-to-all-start.11 = ((f32[64,1,6]{2,1,0:T(1,128)}), f32[64,1,6]{2,1,0:T(1,128)S(1)}, u32[]{:S(2)}, u32[]{:S(2)}) async-start(f32[64,1,6]{2,1,0:T(1,128)} %broadcast_in_dim.79), calls=%async_computation.11 | async-start | bytes 65536 | tf_op jit(solution)/shard_map/all_to_all | solution.py:36
  342.9 11.9 %collective-permute-start.42 = (f32[2,4,8,1]{3,2,1,0:T(8,128)S(1)}, f32[2,4,8,1]{3,2,1,0:T(8,128)S(1)}, u32[]{:S(2)}, u32[]{:S(2)}) collective-permute-start(f32[2,4,8,1]{3,2,1,0:T(8,128)S(1)} %get-tuple-element.1135), channel_id=1, source_target_pairs={{0,1},{1,2},{2,3},{3,4},{4,5},{5,6},{6,7},{8,9},{9,10},{10,11},{11... | collective-permute-start | bytes 776 | tf_op jit(solution)/shard_map/ppermute | solution.py:22
  362.3 10.2 %all-to-all-start.12 = ((f32[8,1,7]{2,1,0:T(1,128)}), f32[8,1,7]{2,1,0:T(1,128)S(1)}, u32[]{:S(2)}, u32[]{:S(2)}) async-start(f32[8,1,7]{2,1,0:T(1,128)} %broadcast_in_dim.80), calls=%async_computation.12 | async-start | bytes 8192 | tf_op jit(solution)/shard_map/all_to_all | solution.py:36
  373.2 18.1 %all-to-all-start.13 = ((f32[64,1,7]{2,1,0:T(1,128)}), f32[64,1,7]{2,1,0:T(1,128)S(1)}, u32[]{:S(2)}, u32[]{:S(2)}) async-start(f32[64,1,7]{2,1,0:T(1,128)} %broadcast_in_dim.81), calls=%async_computation.13 | async-start | bytes 65536 | tf_op jit(solution)/shard_map/all_to_all | solution.py:36
  394.4 12.6 %collective-permute-start.48 = (f32[2,4,8,1]{3,2,1,0:T(8,128)S(1)}, f32[2,4,8,1]{3,2,1,0:T(8,128)S(1)}, u32[]{:S(2)}, u32[]{:S(2)}) collective-permute-start(f32[2,4,8,1]{3,2,1,0:T(8,128)S(1)} %get-tuple-element.1127), channel_id=1, source_target_pairs={{0,1},{1,2},{2,3},{3,4},{4,5},{5,6},{6,7},{8,9},{9,10},{10,11},{11... | collective-permute-start | bytes 776 | tf_op jit(solution)/shard_map/ppermute | solution.py:22
  398.6 13.6 %collective-permute-start.50 = (f32[2,1,8,128]{3,2,1,0:T(8,128)S(1)}, f32[2,1,8,128]{3,2,1,0:T(8,128)S(1)}, u32[]{:S(2)}, u32[]{:S(2)}) collective-permute-start(f32[2,1,8,128]{3,2,1,0:T(8,128)S(1)} %get-tuple-element.1125), channel_id=1, source_target_pairs={{0,64},{64,128},{128,192},{192,256},{256,320},{320,384},{384,448},... | collective-permute-start | bytes 24584 | tf_op jit(solution)/shard_map/ppermute | solution.py:22
  400.9 11.4 %collective-permute-start.51 = (f32[2,1,8,128]{3,2,1,0:T(8,128)S(1)}, f32[2,1,8,128]{3,2,1,0:T(8,128)S(1)}, u32[]{:S(2)}, u32[]{:S(2)}) collective-permute-start(f32[2,1,8,128]{3,2,1,0:T(8,128)S(1)} %get-tuple-element.1126), channel_id=1, source_target_pairs={{64,0},{128,64},{192,128},{256,192},{320,256},{384,320},{448,384},... | collective-permute-start | bytes 24584 | tf_op jit(solution)/shard_map/ppermute | solution.py:23
  424.0 19.6 %all-to-all-start.15 = ((f32[64,1,8]{2,1,0:T(1,128)}), f32[64,1,8]{2,1,0:T(1,128)S(1)}, u32[]{:S(2)}, u32[]{:S(2)}) async-start(f32[64,1,8]{2,1,0:T(1,128)} %broadcast_in_dim.83), calls=%async_computation.15 | async-start | bytes 65536 | tf_op jit(solution)/shard_map/all_to_all | solution.py:36
  446.6 14.8 %collective-permute-start.54 = (f32[2,4,8,1]{3,2,1,0:T(8,128)S(1)}, f32[2,4,8,1]{3,2,1,0:T(8,128)S(1)}, u32[]{:S(2)}, u32[]{:S(2)}) collective-permute-start(f32[2,4,8,1]{3,2,1,0:T(8,128)S(1)} %get-tuple-element.1119), channel_id=1, source_target_pairs={{0,1},{1,2},{2,3},{3,4},{4,5},{5,6},{6,7},{8,9},{9,10},{10,11},{11... | collective-permute-start | bytes 776 | tf_op jit(solution)/shard_map/ppermute | solution.py:22
  451.1 15.6 %collective-permute-start.56 = (f32[2,1,8,128]{3,2,1,0:T(8,128)S(1)}, f32[2,1,8,128]{3,2,1,0:T(8,128)S(1)}, u32[]{:S(2)}, u32[]{:S(2)}) collective-permute-start(f32[2,1,8,128]{3,2,1,0:T(8,128)S(1)} %get-tuple-element.1117), channel_id=1, source_target_pairs={{0,64},{64,128},{128,192},{192,256},{256,320},{320,384},{384,448},... | collective-permute-start | bytes 24584 | tf_op jit(solution)/shard_map/ppermute | solution.py:22
  453.3 13.4 %collective-permute-start.57 = (f32[2,1,8,128]{3,2,1,0:T(8,128)S(1)}, f32[2,1,8,128]{3,2,1,0:T(8,128)S(1)}, u32[]{:S(2)}, u32[]{:S(2)}) collective-permute-start(f32[2,1,8,128]{3,2,1,0:T(8,128)S(1)} %get-tuple-element.1118), channel_id=1, source_target_pairs={{64,0},{128,64},{192,128},{256,192},{320,256},{384,320},{448,384},... | collective-permute-start | bytes 24584 | tf_op jit(solution)/shard_map/ppermute | solution.py:23
  454.6 12.1 %collective-permute-start.55 = (f32[2,4,1,128]{3,2,1,0:T(1,128)S(1)}, f32[2,4,1,128]{3,2,1,0:T(1,128)S(1)}, u32[]{:S(2)}, u32[]{:S(2)}) collective-permute-start(f32[2,4,1,128]{3,2,1,0:T(1,128)S(1)} %get-tuple-element.1121), channel_id=1, source_target_pairs={{0,8},{8,16},{16,24},{24,32},{32,40},{40,48},{48,56},{1,9},{9,17},... | collective-permute-start | bytes 12296 | tf_op jit(solution)/shard_map/ppermute | solution.py:22
  478.4 21.0 %all-to-all-start.17 = ((f32[64,1,9]{2,1,0:T(1,128)}), f32[64,1,9]{2,1,0:T(1,128)S(1)}, u32[]{:S(2)}, u32[]{:S(2)}) async-start(f32[64,1,9]{2,1,0:T(1,128)} %broadcast_in_dim.85), calls=%async_computation.17 | async-start | bytes 65536 | tf_op jit(solution)/shard_map/all_to_all | solution.py:36
  502.4 14.7 %collective-permute-start.60 = (f32[2,4,8,1]{3,2,1,0:T(8,128)S(1)}, f32[2,4,8,1]{3,2,1,0:T(8,128)S(1)}, u32[]{:S(2)}, u32[]{:S(2)}) collective-permute-start(f32[2,4,8,1]{3,2,1,0:T(8,128)S(1)} %get-tuple-element.1111), channel_id=1, source_target_pairs={{0,1},{1,2},{2,3},{3,4},{4,5},{5,6},{6,7},{8,9},{9,10},{10,11},{11... | collective-permute-start | bytes 776 | tf_op jit(solution)/shard_map/ppermute | solution.py:22
  506.6 15.7 %collective-permute-start.62 = (f32[2,1,8,128]{3,2,1,0:T(8,128)S(1)}, f32[2,1,8,128]{3,2,1,0:T(8,128)S(1)}, u32[]{:S(2)}, u32[]{:S(2)}) collective-permute-start(f32[2,1,8,128]{3,2,1,0:T(8,128)S(1)} %get-tuple-element.1109), channel_id=1, source_target_pairs={{0,64},{64,128},{128,192},{192,256},{256,320},{320,384},{384,448},... | collective-permute-start | bytes 24584 | tf_op jit(solution)/shard_map/ppermute | solution.py:22
  508.9 13.5 %collective-permute-start.63 = (f32[2,1,8,128]{3,2,1,0:T(8,128)S(1)}, f32[2,1,8,128]{3,2,1,0:T(8,128)S(1)}, u32[]{:S(2)}, u32[]{:S(2)}) collective-permute-start(f32[2,1,8,128]{3,2,1,0:T(8,128)S(1)} %get-tuple-element.1110), channel_id=1, source_target_pairs={{64,0},{128,64},{192,128},{256,192},{320,256},{384,320},{448,384},... | collective-permute-start | bytes 24584 | tf_op jit(solution)/shard_map/ppermute | solution.py:23
  510.2 12.2 %collective-permute-start.61 = (f32[2,4,1,128]{3,2,1,0:T(1,128)S(1)}, f32[2,4,1,128]{3,2,1,0:T(1,128)S(1)}, u32[]{:S(2)}, u32[]{:S(2)}) collective-permute-start(f32[2,4,1,128]{3,2,1,0:T(1,128)S(1)} %get-tuple-element.1113), channel_id=1, source_target_pairs={{0,8},{8,16},{16,24},{24,32},{32,40},{40,48},{48,56},{1,9},{9,17},... | collective-permute-start | bytes 12296 | tf_op jit(solution)/shard_map/ppermute | solution.py:22
  534.5 20.9 %all-to-all-start.19 = ((f32[64,1,10]{2,1,0:T(1,128)}), f32[64,1,10]{2,1,0:T(1,128)S(1)}, u32[]{:S(2)}, u32[]{:S(2)}) async-start(f32[64,1,10]{2,1,0:T(1,128)} %broadcast_in_dim.87), calls=%async_computation.19 | async-start | bytes 65536 | tf_op jit(solution)/shard_map/all_to_all | solution.py:36
  558.8 14.7 %collective-permute-start.66 = (f32[2,4,8,1]{3,2,1,0:T(8,128)S(1)}, f32[2,4,8,1]{3,2,1,0:T(8,128)S(1)}, u32[]{:S(2)}, u32[]{:S(2)}) collective-permute-start(f32[2,4,8,1]{3,2,1,0:T(8,128)S(1)} %get-tuple-element.1103), channel_id=1, source_target_pairs={{0,1},{1,2},{2,3},{3,4},{4,5},{5,6},{6,7},{8,9},{9,10},{10,11},{11... | collective-permute-start | bytes 776 | tf_op jit(solution)/shard_map/ppermute | solution.py:22
  563.0 15.8 %collective-permute-start.68 = (f32[2,1,8,128]{3,2,1,0:T(8,128)S(1)}, f32[2,1,8,128]{3,2,1,0:T(8,128)S(1)}, u32[]{:S(2)}, u32[]{:S(2)}) collective-permute-start(f32[2,1,8,128]{3,2,1,0:T(8,128)S(1)} %get-tuple-element.1101), channel_id=1, source_target_pairs={{0,64},{64,128},{128,192},{192,256},{256,320},{320,384},{384,448},... | collective-permute-start | bytes 24584 | tf_op jit(solution)/shard_map/ppermute | solution.py:22
  565.2 13.5 %collective-permute-start.69 = (f32[2,1,8,128]{3,2,1,0:T(8,128)S(1)}, f32[2,1,8,128]{3,2,1,0:T(8,128)S(1)}, u32[]{:S(2)}, u32[]{:S(2)}) collective-permute-start(f32[2,1,8,128]{3,2,1,0:T(8,128)S(1)} %get-tuple-element.1102), channel_id=1, source_target_pairs={{64,0},{128,64},{192,128},{256,192},{320,256},{384,320},{448,384},... | collective-permute-start | bytes 24584 | tf_op jit(solution)/shard_map/ppermute | solution.py:23
  566.5 12.2 %collective-permute-start.67 = (f32[2,4,1,128]{3,2,1,0:T(1,128)S(1)}, f32[2,4,1,128]{3,2,1,0:T(1,128)S(1)}, u32[]{:S(2)}, u32[]{:S(2)}) collective-permute-start(f32[2,4,1,128]{3,2,1,0:T(1,128)S(1)} %get-tuple-element.1105), channel_id=1, source_target_pairs={{0,8},{8,16},{16,24},{24,32},{32,40},{40,48},{48,56},{1,9},{9,17},... | collective-permute-start | bytes 12296 | tf_op jit(solution)/shard_map/ppermute | solution.py:22
  591.0 19.6 %all-to-all-start.21 = ((f32[64,1,11]{2,1,0:T(1,128)}), f32[64,1,11]{2,1,0:T(1,128)S(1)}, u32[]{:S(2)}, u32[]{:S(2)}) async-start(f32[64,1,11]{2,1,0:T(1,128)} %broadcast_in_dim.89), calls=%async_computation.21 | async-start | bytes 65536 | tf_op jit(solution)/shard_map/all_to_all | solution.py:36
  (57 other events, 374.3 us)
where the time goes:
time: 724 us; the launch traced here: 711 us
  starting transfers between devices  324 us (45%)
  waiting for transfers between devices  169 us (23%)
  between operations  83 us (11%)
  local copies, waits for them, and re-layouts  64 us (9%)
  other arithmetic  59.3 us (8%)
  matrix products  11.6 us (2%)
    all_to_all x22, starting transfers between devices, copy_for_each(): return lax.all_to_all(copies, axis, split_axis=0, concat_axis=0, tiled=True)  154 us
    all_to_all x22, waiting for transfers between devices, copy_for_each(): return lax.all_to_all(copies, axis, split_axis=0, concat_axis=0, tiled=True)  141 us
    ppermute x36, starting transfers between devices, with_halo(): lax.ppermute(last, axis, up)  111 us
    ppermute x36, starting transfers between devices, with_halo(): lax.ppermute(initial, axis, [(b, a) for a, b in up])  57.8 us
    ppermute x36, waiting for transfers between devices, with_halo(): lax.ppermute(initial, axis, [(b, a) for a, b in up])  28.6 us
    another operation x26, other arithmetic  23.6 us
    scatter x20, local copies, waits for them, and re-layouts, body(): hessenberg.at[:column + 1, column].set(project).at[column + 1, column]  15.1 us
    broadcast_in_dim x22, local copies, waits for them, and re-layouts, copy_for_each(): copies = jnp.broadcast_to(x, (lax.axis_size(axis), *x.shape))  14.9 us
  transfers between devices with their start and end apart: 94, of which 31 were waited for; matrix products, arithmetic and copies ran while one was open for 7% of the time, Pallas kernels for 0%

commit v1 on v0

v1 whole, which is shorter than its diff:
```python
import functools

import jax
import jax.numpy as jnp
from jax import lax
from jax.experimental import pallas as pl
from jax.experimental.pallas import tpu as pltpu
from jax.sharding import PartitionSpec as P

KRYLOV = 10
AXES = ("gx", "gy", "gz")
MESH = pl.DeviceIdType.MESH
NX, NY, NZ = 4, 8, 128
Q = 2 * NX
PAIRS = (KRYLOV + 1) * (KRYLOV + 2) // 2
TILE = (NY, NZ)


def sublane():
    return lax.broadcasted_iota(jnp.int32, TILE, 0)


def lane():
    return lax.broadcasted_iota(jnp.int32, TILE, 1)


def cycle_kernel(
    sizes,
    source_hbm, intra_hbm, extra_hbm, membrane_hbm,
    solution_ref, residual_ref,
    sigma, member, basis, u,
    coef_x, coef_y, coef_z, edge_y, edge_z, block, inverse,
    sigma_gx, sigma_gy, sigma_gz,
    send_x, send_y, send_z, ghost_x, ghost_y, ghost_z,
    gram_rows, gram_all, mine, parts,
    local_sem, sigma_send, sigma_recv, send_sem, recv_sem, sum_send, sum_recv,
):
    where = [lax.axis_index(a) for a in AXES]
    has = [(where[d] > 0, where[d] < sizes[d] - 1) for d in range(3)]

    loads = [
        pltpu.make_async_copy(intra_hbm, sigma.at[0], local_sem.at[0]),
        pltpu.make_async_copy(extra_hbm, sigma.at[1], local_sem.at[1]),
        pltpu.make_async_copy(membrane_hbm, member, local_sem.at[2]),
        pltpu.make_async_copy(source_hbm, basis.at[0], local_sem.at[3]),
    ]
    for c in loads:
        c.start()

    for ref in (sigma_gx, sigma_gy, sigma_gz, ghost_x, ghost_y, ghost_z):
        ref[...] = jnp.zeros_like(ref)
    gram_all[...] = jnp.zeros_like(gram_all)

    barrier = pltpu.get_barrier_semaphore()
    for d in range(3):
        for j in range(1, sizes[d]):
            other = lax.rem(where[d] + j, sizes[d])
            pl.semaphore_signal(barrier, inc=1, device_id={AXES[d]: other}, device_id_type=MESH)
    for k in range(1, KRYLOV + 1):
        basis[k] = jnp.zeros_like(basis.at[k])
    for c in loads:
        c.wait()
    pl.semaphore_wait(barrier, sum(n - 1 for n in sizes))

    def remote(src, dst, ssem, rsem, d, side):
        step = 1 if side else -1
        return pltpu.make_async_remote_copy(
            src_ref=src, dst_ref=dst, send_sem=ssem, recv_sem=rsem,
            device_id={AXES[d]: where[d] + step}, device_id_type=MESH,
        )

    def sigma_copies(d, side):
        made = []
        for s in range(2):
            if d == 0:
                src, dst = sigma.at[s, 0, NX - 1 if side else 0], sigma_gx.at[1 - side, s]
            elif d == 1:
                row = NY - 1 if side else 0
                src, dst = sigma.at[s, 1, :, pl.ds(row, 1), :], sigma_gy.at[1 - side, s, :, pl.ds(0, 1), :]
            else:
                src, dst = sigma.at[s, 2], sigma_gz.at[1 - side, s]
            made.append(
                remote(src, dst, sigma_send.at[d, side, s], sigma_recv.at[d, 1 - side, s], d, side)
            )
        return made

    for d in range(3):
        for side in range(2):
            @pl.when(has[d][side])
            def _():
                for c in sigma_copies(d, side):
                    c.start()
    for d in range(3):
        for side in range(2):
            @pl.when(has[d][side])
            def _():
                for c in sigma_copies(d, side):
                    c.wait_send()
                for c in sigma_copies(d, 1 - side):
                    c.wait_recv()

    row, col = sublane(), lane()
    first_row, last_row = row == 0, row == NY - 1
    first_col, last_col = col == 0, col == NZ - 1
    diagonals = []
    for s in range(2):
        across = [sigma_gx[0, s]] + [sigma[s, 0, x] for x in range(NX)] + [sigma_gx[1, s]]
        total = []
        for x in range(NX):
            upper = 0.5 * (across[x + 1] + across[x + 2])
            lower = 0.5 * (across[x + 1] + across[x])
            coef_x[s, 0, x] = lower
            coef_x[s, 1, x] = upper
            diagonal = upper + lower
            here = sigma[s, 1, x]
            ahead = jnp.where(last_row, sigma_gy[1, s, x, 0:1, :], pltpu.roll(here, NY - 1, 0))
            behind = jnp.where(first_row, sigma_gy[0, s, x, 0:1, :], pltpu.roll(here, 1, 0))
            upper = 0.5 * (here + ahead)
            lower = 0.5 * (here + behind)
            coef_y[s, 0, x] = jnp.where(first_row, 0.0, lower)
            coef_y[s, 1, x] = jnp.where(last_row, 0.0, upper)
            edge_y[s, x] = jnp.where(first_row, lower, jnp.where(last_row, upper, 0.0))
            diagonal = diagonal + upper + lower
            here = sigma[s, 2, x]
            ahead = jnp.where(last_col, pltpu.roll(sigma_gz[1, s, x], NZ - 1, 1), pltpu.roll(here, NZ - 1, 1))
            behind = jnp.where(first_col, pltpu.roll(sigma_gz[0, s, x], 1, 1), pltpu.roll(here, 1, 1))
            upper = 0.5 * (here + ahead)
            lower = 0.5 * (here + behind)
            coef_z[s, 0, x] = jnp.where(first_col, 0.0, lower)
            coef_z[s, 1, x] = jnp.where(last_col, 0.0, upper)
            edge_z[s, x] = jnp.where(first_col, lower, jnp.where(last_col, upper, 0.0))
            total.append(diagonal + upper + lower)
        diagonals.append(total)
    for x in range(NX):
        di, de, m = diagonals[0][x], diagonals[1][x], member[x]
        det = m * di + m * de + di * de
        inverse[0, x] = (di + de) / det
        inverse[1, x] = -di / det
        inverse[2, x] = (m + di) / det
        block[0, x] = de / det
        block[1, x] = m / det

    def solved(v):
        joined, second = [], []
        for x in range(NX):
            a, b = v[x], v[NX + x]
            joined.append(block[0, x] * a + block[1, x] * b)
            second.append(inverse[1, x] * a + inverse[2, x] * b)
        return joined + second

    def stage(values):
        lo = values[0]
        hi = values[0]
        for q in range(Q):
            u[q] = values[q]
            send_y[0, pl.ds(q, 1), :] = values[q][0:1, :]
            send_y[1, pl.ds(q, 1), :] = values[q][NY - 1 : NY, :]
            low = pltpu.roll(values[q], 2 * q, 1) if q else values[q]
            high = pltpu.roll(values[q], 2 * q + 2, 1)
            lo = low if q == 0 else jnp.where(col == 2 * q, low, lo)
            hi = high if q == 0 else jnp.where(col == 2 * q + 1, high, hi)
        send_z[0] = lo
        send_z[1] = hi
        for s in range(2):
            send_x[0, s] = values[s * NX]
            send_x[1, s] = values[s * NX + NX - 1]

    def halo(slot, d, side):
        send = (send_x, send_y, send_z)[d]
        ghost = (ghost_x, ghost_y, ghost_z)[d]
        return remote(
            send.at[side], ghost.at[slot, 1 - side],
            send_sem.at[d, side], recv_sem.at[slot, d, 1 - side], d, side,
        )

    def start(slot):
        for d in (2, 0, 1):
            for side in range(2):
                @pl.when(has[d][side])
                def _():
                    halo(slot, d, side).start()

    def finish(slot):
        for d in (0, 1, 2):
            for side in range(2):
                @pl.when(has[d][side])
                def _():
                    halo(slot, d, side).wait_send()
                    halo(slot, d, 1 - side).wait_recv()

    def gram_row(k):
        at = [basis[k, q // NX, q % NX] for q in range(Q)]
        for i in range(KRYLOV + 1):
            total = at[0] * basis[i, 0, 0]
            for q in range(1, Q):
                total = total + at[q] * basis[i, q // NX, q % NX]
            gram_rows[k, pl.ds(i, 1), :] = jnp.sum(total, axis=0, keepdims=True)

    def inner(s, x):
        field = u[s * NX + x]
        r = coef_y[s, 0, x] * pltpu.roll(field, 1, 0) + coef_y[s, 1, x] * pltpu.roll(field, NY - 1, 0)
        r = r + coef_z[s, 0, x] * pltpu.roll(field, 1, 1) + coef_z[s, 1, x] * pltpu.roll(field, NZ - 1, 1)
        if x > 0:
            r = r + coef_x[s, 0, x] * u[s * NX + x - 1]
        if x < NX - 1:
            r = r + coef_x[s, 1, x] * u[s * NX + x + 1]
        return r

    def advance(k, slot, twice, previous):
        partial = [inner(s, x) for s in range(2) for x in range(NX)]
        gram_row(k)
        finish(slot)
        beside = jnp.where(lax.rem(col, 2) == 1, ghost_z[slot, 0], ghost_z[slot, 1])
        off = []
        for s in range(2):
            for x in range(NX):
                q = s * NX + x
                r = partial[q]
                if x == 0:
                    r = r + coef_x[s, 0, x] * ghost_x[slot, 0, s]
                if x == NX - 1:
                    r = r + coef_x[s, 1, x] * ghost_x[slot, 1, s]
                rows = jnp.where(row < NY // 2, ghost_y[slot, 0, pl.ds(q, 1), :], ghost_y[slot, 1, pl.ds(q, 1), :])
                r = r + edge_y[s, x] * rows
                r = r + edge_z[s, x] * pltpu.roll(beside, NZ - (2 * q + 1), 1)
                off.append(r)
        new = [off[x] for x in range(NX)] + [off[x] + off[NX + x] for x in range(NX)]
        if twice:
            new = [2.0 * new[q] - basis[previous, q // NX, q % NX] for q in range(Q)]
        return new

    def keep(k, v):
        for q in range(Q):
            basis[k, q // NX, q % NX] = v[q]

    stage(solved([basis[0, q // NX, q % NX] for q in range(Q)]))
    start(0)
    v = advance(0, 0, False, None)
    stage(solved(v))
    start(1)
    keep(1, v)

    def step(k, carry):
        slot = lax.rem(k, 2)
        v = advance(k, slot, True, k - 1)
        stage(solved(v))
        start(1 - slot)
        keep(k + 1, v)
        return carry

    lax.fori_loop(1, KRYLOV - 1, step, 0)
    keep(KRYLOV, advance(KRYLOV - 1, (KRYLOV - 1) % 2, True, KRYLOV - 2))
    gram_row(KRYLOV)

    at = 0
    for k in range(KRYLOV + 1):
        gram_all[pl.ds(at, k + 1), :] = gram_rows[k, pl.ds(0, k + 1), :]
        at += k + 1
    summed = lax.dot_general(
        jnp.ones(TILE, jnp.float32), gram_all[...], (((1,), (1,)), ((), ())),
        precision=lax.Precision.HIGHEST, preferred_element_type=jnp.float32,
    )
    for n, d in enumerate((2, 1, 0)):
        size = sizes[d]
        mine[n, 0:1, :] = summed[0:1, :]
        parts[n, where[d], 0:1, :] = summed[0:1, :]

        def copy(j):
            other = lax.rem(where[d] + j, size)
            return pltpu.make_async_remote_copy(
                src_ref=mine.at[n, pl.ds(0, 1), :], dst_ref=parts.at[n, where[d], pl.ds(0, 1), :],
                send_sem=sum_send.at[n, j], recv_sem=sum_recv.at[n, where[d]],
                device_id={AXES[d]: other}, device_id_type=MESH,
            )

        def arrival(j):
            other = lax.rem(where[d] + j, size)
            return pltpu.make_async_remote_copy(
                src_ref=mine.at[n, pl.ds(0, 1), :], dst_ref=parts.at[n, other, pl.ds(0, 1), :],
                send_sem=sum_send.at[n, j], recv_sem=sum_recv.at[n, other],
                device_id={AXES[d]: other}, device_id_type=MESH,
            )

        for j in range(1, size):
            copy(j).start()
        for j in range(1, size):
            arrival(j).wait_recv()
        for j in range(1, size):
            copy(j).wait_send()
        terms = [parts[n, j, 0:1, :] for j in range(size)]
        while len(terms) > 1:
            terms = [terms[i] + terms[i + 1] for i in range(0, len(terms), 2)]
        summed = terms[0]

    g = {}
    at = 0
    for k in range(KRYLOV + 1):
        for i in range(k + 1):
            g[k, i] = jnp.broadcast_to(summed[:, at : at + 1], TILE)
            at += 1
    size = KRYLOV + 1
    right = [jnp.ones(TILE, jnp.float32) for _ in range(size)]
    over = []
    for k in range(size):
        over.append(1.0 / g[k, k])
        for i in range(k + 1, size):
            factor = g[i, k] * over[k]
            for j in range(k + 1, i + 1):
                g[i, j] = g[i, j] - factor * g[j, k]
            right[i] = right[i] - factor * right[k]
    z = [None] * size
    for k in range(size - 1, -1, -1):
        rest = right[k]
        for j in range(k + 1, size):
            rest = rest - g[j, k] * z[j]
        z[k] = rest * over[k]
    total = z[0]
    for k in range(1, size):
        total = total + z[k]
    scale = 1.0 / total
    rho = [scale * a for a in z]
    tail, slope = [None] * size, [None] * size
    running = jnp.zeros(TILE, jnp.float32)
    weighted = jnp.zeros(TILE, jnp.float32)
    for j in range(KRYLOV - 1, -1, -1):
        running = running + rho[j + 1]
        weighted = weighted + running
        slope[j] = weighted
    coeffs = [slope[0]] + [2.0 * slope[j] for j in range(1, KRYLOV)]

    for x in range(NX):
        left, below = [], []
        for s in range(2):
            vectors = [basis[k, s, x] for k in range(size)]
            r = rho[0] * vectors[0]
            c = coeffs[0] * vectors[0]
            for k in range(1, size):
                r = r + rho[k] * vectors[k]
                if k < KRYLOV:
                    c = c + coeffs[k] * vectors[k]
            residual_ref[s, x] = r
            left.append(c)
        solution_ref[0, x] = inverse[0, x] * left[0] + inverse[1, x] * left[1]
        solution_ref[1, x] = inverse[1, x] * left[0] + inverse[2, x] * left[1]


def body(source, sigma_intra, sigma_extra, membrane):
    sizes = tuple(lax.axis_size(a) for a in AXES)
    f32 = jnp.float32
    vm = lambda *s: pltpu.VMEM(s, f32)
    dma = pltpu.SemaphoreType.DMA
    out = jax.ShapeDtypeStruct(source.shape, f32)
    return pl.pallas_call(
        functools.partial(cycle_kernel, sizes),
        out_shape=(out, out),
        in_specs=[pl.BlockSpec(memory_space=pl.ANY)] * 4,
        out_specs=(pl.BlockSpec(memory_space=pltpu.VMEM),) * 2,
        scratch_shapes=[
            vm(2, 3, NX, *TILE), vm(NX, *TILE), vm(KRYLOV + 1, 2, NX, *TILE), vm(Q, *TILE),
            vm(2, 2, NX, *TILE), vm(2, 2, NX, *TILE), vm(2, 2, NX, *TILE),
            vm(2, NX, *TILE), vm(2, NX, *TILE), vm(2, NX, *TILE), vm(3, NX, *TILE),
            vm(2, 2, *TILE), vm(2, 2, NX, *TILE), vm(2, 2, NX, *TILE),
            vm(2, 2, *TILE), vm(2, *TILE), vm(2, *TILE),
            vm(2, 2, 2, *TILE), vm(2, 2, *TILE), vm(2, 2, *TILE),
            vm(KRYLOV + 1, 16, NZ), vm(128, NZ), vm(3, *TILE), vm(3, 8, *TILE),
            dma((4,)), dma((3, 2, 2)), dma((3, 2, 2)), dma((3, 2)), dma((2, 3, 2)),
            dma((3, 8)), dma((3, 8)),
        ],
        compiler_params=pltpu.CompilerParams(collective_id=0, has_side_effects=True),
    )(source, sigma_intra, sigma_extra, membrane)


def solution(mesh):
    return jax.shard_map(
        body,
        mesh=mesh,
        in_specs=(
            P(None, "gx", "gy", "gz"),
            P(None, "gx", "gy", "gz"),
            P(None, "gx", "gy", "gz"),
            P("gx", "gy", "gz"),
        ),
        out_specs=(P(None, "gx", "gy", "gz"), P(None, "gx", "gy", "gz")),
        check_vma=False,
    )
```

time: 724 us -> 69.3 us (0.10); the launches traced: 711 us -> 69.1 us
  starting transfers between devices: 324 us -> 0 us
  waiting for transfers between devices: 169 us -> 0 us
  between operations: 83 us -> 0.65 us
  Pallas kernels: 0 us -> 66.4 us
  local copies, waits for them, and re-layouts: 64 us -> 2 us
  other arithmetic: 59.3 us -> 0 us
  matrix products: 11.6 us -> 0 us
    ppermute x72 -> x0, starting transfers between devices: 169 us -> none  [the longest x36 111 us: with_halo(): lax.ppermute(last, axis, up)]
    all_to_all x22 -> x0, starting transfers between devices: 154 us -> none  [copy_for_each(): return lax.all_to_all(copies, axis, split_axis=0, concat_axis=0, tiled=True)]
    all_to_all x22 -> x0, waiting for transfers between devices: 141 us -> none  [copy_for_each(): return lax.all_to_all(copies, axis, split_axis=0, concat_axis=0, tiled=True)]
    pallas_call x0 -> x1, Pallas kernels: none -> 66.4 us  [body(): pl.pallas_call(functools.partial(cycle_kernel, sizes), out_shape=(out, ou...]
    another operation x58 -> x0, other arithmetic: 31.7 us -> none
    ppermute x72 -> x0, waiting for transfers between devices: 28.7 us -> none  [the longest x36 28.6 us: with_halo(): lax.ppermute(initial, axis, [(b, a) for a, b in up])]
    slice x90 -> x0, local copies, waits for them, and re-layouts: 24.2 us -> none  [the longest x10 5.84 us: packed_total(): done.append(so_far[at:at + a.size].reshape(a.shape))]
    scatter x58 -> x0, local copies, waits for them, and re-layouts: 16.6 us -> none  [the longest x20 15.1 us: body(): hessenberg.at[:column + 1, column].set(project).at[column + 1, column]]
  transfers between devices with their start and end apart: 94 -> 0, of which waited for: 31 -> 0; matrix products, arithmetic and copies ran while one was open for 7% -> 0% of each run, Pallas kernels for 0% -> 0%
where the time goes in v1:
time: 69.3 us; the launch traced here: 69.1 us
  Pallas kernels  66.4 us (96%)
  local copies, waits for them, and re-layouts  2 us (3%)
    pallas_call x1, Pallas kernels, body(): pl.pallas_call(functools.partial(cycle_kernel, sizes), out_shape=(out, ou...  66.4 us
    unnamed x4, local copies, waits for them, and re-layouts  2 us

profile of v1, /device:TPU:1, one launch (start us, length us, event | category | flops | bytes accessed | tf_op | source)
XLA Modules:
  0.0 69.1 jit_solution(12274892834194427698)
XLA Ops:
  0.6 66.4 %shard_map.59 = (f32[2,4,8,128]{3,2,1,0:T(8,128)}, f32[2,4,8,128]{3,2,1,0:T(8,128)}) custom-call(f32[2,4,8,128]{3,2,1,0:T(8,128)} %source_hbm.1, f32[3,4,8,128]{3,2,1,0:T(8,128)} %intra_hbm.1, f32[3,4,8,128]{3,2,1,0:T(8,128)} %extra_hbm.1, f32[4,8,128]{2,1,0:T(8,128)} %membrane_hbm.1), custom_call_target="tpu_custom_call" | custom-call | tf_op jit(solution)/shard_map/pallas_call | solution.py:353
  67.1 0.0 copy-start
  67.1 1.4 %copy.8 = f32[2,4,8,128]{3,2,1,0:T(8,128)} copy(f32[2,4,8,128]{3,2,1,0:T(8,128)} %get-tuple-element.4) | data formatting | bytes 65536
  68.5 0.0 copy-done
  68.5 0.6 copy.9
Async XLA Ops:
  67.1 1.4 %copy-start = (f32[2,4,8,128]{3,2,1,0:T(8,128)S(1)}, f32[2,4,8,128]{3,2,1,0:T(8,128)}, u32[]{:S(2)}) copy-start(f32[2,4,8,128]{3,2,1,0:T(8,128)} %get-tuple-element.5) | copy-start | bytes 98308

commit v2 on v1

v2 whole, which is shorter than its diff:
```python
import functools
import itertools

import jax
import jax.numpy as jnp
from jax import lax
from jax.experimental import pallas as pl
from jax.experimental.pallas import tpu as pltpu
from jax.sharding import PartitionSpec as P

KRYLOV = 10
AXES = ("gx", "gy", "gz")
MESH = pl.DeviceIdType.MESH
NX, NY, NZ = 4, 8, 128
PAIRS = (KRYLOV + 1) * (KRYLOV + 2) // 2
TILE = (NY, NZ)
OWN, BESIDE = 0, 1
DIRECTIONS = [
    d for d in itertools.product((-1, 0, 1), repeat=3) if 1 <= sum(abs(a) for a in d) <= 2
]
TILES = (
    [(x, OWN, OWN) for x in range(-1, NX + 1)]
    + [(x, BESIDE, OWN) for x in range(NX)]
    + [(x, OWN, BESIDE) for x in range(NX)]
)
PLACE = {t: n for n, t in enumerate(TILES)}
FIELDS = 7


class Halo:
    def __init__(self, refs, fields, where, sizes):
        (self.own, self.pack, self.gx, self.gy, self.gz, self.gxy, self.gxz, self.gyz,
         self.send_sem, self.recv_sem) = refs
        self.fields, self.where, self.sizes = fields, where, sizes

    def exists(self, direction):
        there = None
        for axis, step in enumerate(direction):
            if step:
                at = self.where[axis]
                ok = at > 0 if step < 0 else at < self.sizes[axis] - 1
                there = ok if there is None else jnp.logical_and(there, ok)
        return there

    def copy(self, slot, direction):
        n = DIRECTIONS.index(direction)
        dx, dy, dz = direction
        ghost_x, ghost_z = (0 if dx > 0 else 1), (0 if dz > 0 else 1)
        row = NY - 1 if dy > 0 else 0
        if dx and dy:
            src = self.own.at[:, NX - 1 if dx > 0 else 0, pl.ds(row, 1), :]
            dst = self.gxy.at[slot, ghost_x, :, pl.ds(row, 1), :]
        elif dx and dz:
            src, dst = self.pack.at[...], self.gxz.at[slot, ghost_x, ghost_z]
        elif dy and dz:
            src = self.pack.at[pl.ds(row, 1), :]
            dst = self.gyz.at[slot, ghost_z, pl.ds(row, 1), :]
        elif dx:
            src = self.own.at[:, pl.ds(NX - 2 if dx > 0 else 0, 2)]
            dst = self.gx.at[slot, ghost_x]
        elif dy:
            rows = pl.ds(NY - 2 if dy > 0 else 0, 2)
            src, dst = self.own.at[:, :, rows, :], self.gy.at[slot, :, :, rows, :]
        else:
            src, dst = self.pack.at[...], self.gz.at[slot, ghost_z]
        return pltpu.make_async_remote_copy(
            src_ref=src, dst_ref=dst,
            send_sem=self.send_sem.at[n], recv_sem=self.recv_sem.at[slot, n],
            device_id={AXES[a]: self.where[a] + step for a, step in enumerate(direction) if step},
            device_id_type=MESH,
        )

    def fill_pack(self, values):
        group = lax.broadcasted_iota(jnp.int32, TILE, 1) // 4
        packed = None
        for q, v in enumerate(values):
            moved = pltpu.roll(v, 4 * q + 2, 1)
            packed = moved if packed is None else jnp.where(group == q, moved, packed)
        self.pack[...] = packed

    def start(self, slot):
        order = sorted(DIRECTIONS, key=lambda d: -sum(abs(a) for a in d))
        for d in order:
            @pl.when(self.exists(d))
            def _(d=d):
                self.copy(slot, d).start()

    def finish(self, slot):
        for d in DIRECTIONS:
            @pl.when(self.exists(d))
            def _(d=d):
                self.copy(slot, d).wait_send()
        order = sorted(DIRECTIONS, key=lambda d: sum(abs(a) for a in d))
        for d in order:
            @pl.when(self.exists(tuple(-a for a in d)))
            def _(d=d):
                self.copy(slot, d).wait_recv()

    def view(self, slot):
        return View(self, slot)


class View:
    def __init__(self, halo, slot):
        pair = lax.broadcasted_iota(jnp.int32, TILE, 1) % 4 < 2
        self.halo, self.slot, self.made = halo, slot, {}
        merge = lambda ref, *at: jnp.where(pair, ref[(slot, *at, 0)], ref[(slot, *at, 1)])
        self.wz = merge(halo.gz)
        self.wx = [merge(halo.gxz, 0), merge(halo.gxz, 1)]
        self.wy = merge(halo.gyz)

    def tile(self, f, x, ty, tz, turn=0):
        key = (f, x, ty, tz, turn)
        if key not in self.made:
            self.made[key] = self.make(f, x, ty, tz, turn)
        return self.made[key]

    def make(self, f, x, ty, tz, turn):
        h = self.halo
        if tz == BESIDE:
            if ty == BESIDE:
                source, plane = self.wy, x
            elif x < 0:
                source, plane = self.wx[0], NX - 1
            elif x >= NX:
                source, plane = self.wx[1], 0
            else:
                source, plane = self.wz, x
            return pltpu.roll(source, (NZ - (4 * (f * NX + plane) + 2) + turn) % NZ, 1)
        if turn:
            return pltpu.roll(self.tile(f, x, ty, tz), turn % NZ, 1)
        if ty == BESIDE:
            if x < 0:
                return h.gxy[self.slot, 0, f]
            if x >= NX:
                return h.gxy[self.slot, 1, f]
            return h.gy[self.slot, f, x]
        if x < 0:
            return h.gx[self.slot, 0, f, x + 2]
        if x >= NX:
            return h.gx[self.slot, 1, f, x - NX]
        return h.own[f, x]


class Values:
    def __init__(self, values):
        self.values, self.made = values, {}

    def tile(self, f, x, ty, tz, turn=0):
        v = self.values[f][x, ty, tz]
        if not turn:
            return v
        key = (f, x, ty, tz, turn)
        if key not in self.made:
            self.made[key] = pltpu.roll(v, turn % NZ, 1)
        return self.made[key]


def beside(view, f, t, axis, step):
    x, ty, tz = t
    if axis == 0:
        return view.tile(f, x + step, ty, tz)
    if axis == 1:
        edge = lax.broadcasted_iota(jnp.int32, TILE, 0) == (0 if step < 0 else NY - 1)
        shift = 1 if step < 0 else NY - 1
        return jnp.where(
            edge,
            pltpu.roll(view.tile(f, x, 1 - ty, tz), shift, 0),
            pltpu.roll(view.tile(f, x, ty, tz), shift, 0),
        )
    edge = lax.broadcasted_iota(jnp.int32, TILE, 1) == (0 if step < 0 else NZ - 1)
    return jnp.where(edge, view.tile(f, x, ty, 1 - tz, -step), view.tile(f, x, ty, tz, -step))


def cycle_kernel(
    sizes,
    source_hbm, intra_hbm, extra_hbm, membrane_hbm,
    solution_ref, residual_ref,
    basis, coef, block, inverse,
    s_own, s_pack, s_gx, s_gy, s_gz, s_gxy, s_gxz, s_gyz, s_send, s_recv,
    u_own, u_pack, u_gx, u_gy, u_gz, u_gxy, u_gxz, u_gyz, u_send, u_recv,
    gram_rows, gram_all, mine, parts,
    local_sem, sum_send, sum_recv,
):
    where = [lax.axis_index(a) for a in AXES]
    cells = Halo(
        (s_own, s_pack, s_gx, s_gy, s_gz, s_gxy, s_gxz, s_gyz, s_send, s_recv), FIELDS, where, sizes
    )
    halo = Halo(
        (u_own, u_pack, u_gx, u_gy, u_gz, u_gxy, u_gxz, u_gyz, u_send, u_recv), 2, where, sizes
    )

    loads = [
        pltpu.make_async_copy(intra_hbm, s_own.at[pl.ds(0, 3)], local_sem.at[0]),
        pltpu.make_async_copy(extra_hbm, s_own.at[pl.ds(3, 3)], local_sem.at[1]),
        pltpu.make_async_copy(membrane_hbm, s_own.at[6], local_sem.at[2]),
        pltpu.make_async_copy(source_hbm, basis.at[0], local_sem.at[3]),
    ]
    for c in loads:
        c.start()
    for h in (cells, halo):
        for ref in (h.gx, h.gy, h.gz, h.gxy, h.gxz, h.gyz):
            ref[...] = jnp.zeros_like(ref)

    barrier = pltpu.get_barrier_semaphore()
    expected = 0
    for d in DIRECTIONS:
        there = cells.exists(d)
        expected = expected + jnp.where(there, 1, 0)

        @pl.when(there)
        def _(d=d):
            pl.semaphore_signal(
                barrier, inc=1,
                device_id={AXES[a]: where[a] + step for a, step in enumerate(d) if step},
                device_id_type=MESH,
            )
    for d in range(3):
        for j in range(1, sizes[d]):
            other = lax.rem(where[d] + j, sizes[d])
            pl.semaphore_signal(barrier, inc=1, device_id={AXES[d]: other}, device_id_type=MESH)
    gram_all[...] = jnp.zeros_like(gram_all)
    for k in range(1, KRYLOV + 1):
        basis[k] = jnp.zeros_like(basis.at[k])
    for c in loads:
        c.wait()
    cells.fill_pack([s_own[f, x] for f in range(FIELDS) for x in range(NX)])
    pl.semaphore_wait(barrier, expected + sum(n - 1 for n in sizes))

    cells.start(0)
    cells.finish(0)
    view = cells.view(0)
    for t in TILES:
        n = PLACE[t]
        diagonals = []
        for s in range(2):
            total = None
            for axis in range(3):
                here = view.tile(3 * s + axis, *t)
                lower = 0.5 * (here + beside(view, 3 * s + axis, t, axis, -1))
                upper = 0.5 * (here + beside(view, 3 * s + axis, t, axis, 1))
                coef[s, n, 2 * axis] = lower
                coef[s, n, 2 * axis + 1] = upper
                total = upper + lower if total is None else total + upper + lower
            diagonals.append(total)
        di, de, m = diagonals[0], diagonals[1], view.tile(6, *t)
        det = m * di + m * de + di * de
        inside = m > 0.0
        over = jnp.where(inside, 1.0 / jnp.where(inside, det, 1.0), 0.0)
        block[n, 0] = de * over
        block[n, 1] = m * over
        block[n, 2] = -di * over
        block[n, 3] = (m + di) * over
        if n in range(1, NX + 1):
            inverse[n - 1] = (di + de) * over

    def solved(t, a, b):
        n = PLACE[t]
        return block[n, 0] * a + block[n, 1] * b, block[n, 2] * a + block[n, 3] * b

    def apply(view, t):
        n = PLACE[t]
        off = []
        for s in range(2):
            total = None
            for axis in range(3):
                for side, step in enumerate((-1, 1)):
                    term = coef[s, n, 2 * axis + side] * beside(view, s, t, axis, step)
                    total = term if total is None else total + term
            off.append(total)
        return off[0], off[0] + off[1]

    own = [(x, OWN, OWN) for x in range(NX)]

    def load(k):
        return [[basis[k, s, x] for x in range(NX)] for s in range(2)]

    def keep(k, v):
        for s in range(2):
            for x in range(NX):
                basis[k, s, x] = v[s][x]

    def stage(v):
        values = [[None] * NX for _ in range(2)]
        for x in range(NX):
            values[0][x], values[1][x] = solved(own[x], v[0][x], v[1][x])
        for s in range(2):
            for x in range(NX):
                u_own[s, x] = values[s][x]
        halo.fill_pack(values[0] + values[1])

    def gram_row(k):
        at = load(k)
        for i in range(KRYLOV + 1):
            total = None
            for s in range(2):
                for x in range(NX):
                    term = at[s][x] * basis[i, s, x]
                    total = term if total is None else total + term
            gram_rows[k, pl.ds(i, 1), :] = jnp.sum(total, axis=0, keepdims=True)

    def two_steps(slot):
        view = halo.view(slot)
        first, next_u = {}, [{}, {}]
        for t in TILES:
            first[t] = apply(view, t)
            next_u[0][t], next_u[1][t] = solved(t, *first[t])
        values = Values(next_u)
        second = [apply(values, t) for t in own]
        return (
            [[first[t][s] for t in own] for s in range(2)],
            [[second[x][s] for x in range(NX)] for s in range(2)],
        )

    every = [(s, x) for s in range(2) for x in range(NX)]

    def combine(f, *vs):
        return [[f(*(v[s][x] for v in vs)) for x in range(NX)] for s in range(2)]

    def advance(k, slot):
        w, b = two_steps(slot)
        odd = combine(lambda p, q: 2.0 * p - q, w, load(k - 1))
        even = combine(lambda p, q, r: 4.0 * p - 2.0 * q - r, b, load(k), load(k - 2))
        return odd, even

    stage(load(0))
    halo.start(0)
    gram_row(0)
    halo.finish(0)
    odd, b = two_steps(0)
    even = combine(lambda p, q: 2.0 * p - q, b, load(0))
    stage(even)
    halo.start(1)
    keep(1, odd)
    keep(2, even)

    def step(r, carry):
        k, slot = 2 * r, lax.rem(r, 2)
        gram_row(k - 1)
        gram_row(k)
        halo.finish(slot)
        odd, even = advance(k, slot)
        stage(even)
        halo.start(1 - slot)
        keep(k + 1, odd)
        keep(k + 2, even)
        return carry

    rounds = KRYLOV // 2
    lax.fori_loop(1, rounds - 1, step, 0)
    gram_row(KRYLOV - 3)
    gram_row(KRYLOV - 2)
    last = (rounds - 1) % 2
    halo.finish(last)
    odd, even = advance(KRYLOV - 2, last)
    keep(KRYLOV - 1, odd)
    keep(KRYLOV, even)
    gram_row(KRYLOV - 1)
    gram_row(KRYLOV)

    at = 0
    for k in range(KRYLOV + 1):
        gram_all[pl.ds(at, k + 1), :] = gram_rows[k, pl.ds(0, k + 1), :]
        at += k + 1
    summed = lax.dot_general(
        jnp.ones(TILE, jnp.float32), gram_all[...], (((1,), (1,)), ((), ())),
        precision=lax.Precision.HIGHEST, preferred_element_type=jnp.float32,
    )
    for n, d in enumerate((2, 1, 0)):
        size = sizes[d]
        mine[n, 0:1, :] = summed[0:1, :]
        parts[n, where[d], 0:1, :] = summed[0:1, :]

        def copy(j):
            other = lax.rem(where[d] + j, size)
            return pltpu.make_async_remote_copy(
                src_ref=mine.at[n, pl.ds(0, 1), :], dst_ref=parts.at[n, where[d], pl.ds(0, 1), :],
                send_sem=sum_send.at[n, j], recv_sem=sum_recv.at[n, where[d]],
                device_id={AXES[d]: other}, device_id_type=MESH,
            )

        def arrival(j):
            other = lax.rem(where[d] + j, size)
            return pltpu.make_async_remote_copy(
                src_ref=mine.at[n, pl.ds(0, 1), :], dst_ref=parts.at[n, other, pl.ds(0, 1), :],
                send_sem=sum_send.at[n, j], recv_sem=sum_recv.at[n, other],
                device_id={AXES[d]: other}, device_id_type=MESH,
            )

        for j in range(1, size):
            copy(j).start()
        for j in range(1, size):
            arrival(j).wait_recv()
        for j in range(1, size):
            copy(j).wait_send()
        terms = [parts[n, j, 0:1, :] for j in range(size)]
        while len(terms) > 1:
            terms = [terms[i] + terms[i + 1] for i in range(0, len(terms), 2)]
        summed = terms[0]

    g = {}
    at = 0
    for k in range(KRYLOV + 1):
        for i in range(k + 1):
            g[k, i] = jnp.broadcast_to(summed[:, at : at + 1], TILE)
            at += 1
    size = KRYLOV + 1
    right = [jnp.ones(TILE, jnp.float32) for _ in range(size)]
    over = []
    for k in range(size):
        over.append(1.0 / g[k, k])
        for i in range(k + 1, size):
            factor = g[i, k] * over[k]
            for j in range(k + 1, i + 1):
                g[i, j] = g[i, j] - factor * g[j, k]
            right[i] = right[i] - factor * right[k]
    z = [None] * size
    for k in range(size - 1, -1, -1):
        rest = right[k]
        for j in range(k + 1, size):
            rest = rest - g[j, k] * z[j]
        z[k] = rest * over[k]
    total = z[0]
    for k in range(1, size):
        total = total + z[k]
    scale = 1.0 / total
    rho = [scale * a for a in z]
    slope = [None] * size
    running = jnp.zeros(TILE, jnp.float32)
    weighted = jnp.zeros(TILE, jnp.float32)
    for j in range(KRYLOV - 1, -1, -1):
        running = running + rho[j + 1]
        weighted = weighted + running
        slope[j] = weighted
    coeffs = [slope[0]] + [2.0 * slope[j] for j in range(1, KRYLOV)]

    for x in range(NX):
        combined = []
        for s in range(2):
            vectors = [basis[k, s, x] for k in range(size)]
            r = rho[0] * vectors[0]
            c = coeffs[0] * vectors[0]
            for k in range(1, size):
                r = r + rho[k] * vectors[k]
                if k < KRYLOV:
                    c = c + coeffs[k] * vectors[k]
            residual_ref[s, x] = r
            combined.append(c)
        n = PLACE[own[x]]
        solution_ref[0, x] = inverse[x] * combined[0] + block[n, 2] * combined[1]
        solution_ref[1, x] = block[n, 2] * combined[0] + block[n, 3] * combined[1]


def halo_scratch(fields, slots):
    vm = lambda *s: pltpu.VMEM(s, jnp.float32)
    dma = pltpu.SemaphoreType.DMA
    count = len(DIRECTIONS)
    return [
        vm(fields, NX, *TILE), vm(*TILE),
        vm(slots, 2, fields, 2, *TILE), vm(slots, fields, NX, *TILE), vm(slots, 2, *TILE),
        vm(slots, 2, fields, *TILE), vm(slots, 2, 2, *TILE), vm(slots, 2, *TILE),
        dma((count,)), dma((slots, count)),
    ]


def body(source, sigma_intra, sigma_extra, membrane):
    sizes = tuple(lax.axis_size(a) for a in AXES)
    f32 = jnp.float32
    vm = lambda *s: pltpu.VMEM(s, f32)
    dma = pltpu.SemaphoreType.DMA
    out = jax.ShapeDtypeStruct(source.shape, f32)
    count = len(TILES)
    return pl.pallas_call(
        functools.partial(cycle_kernel, sizes),
        out_shape=(out, out),
        in_specs=[pl.BlockSpec(memory_space=pl.ANY)] * 4,
        out_specs=(pl.BlockSpec(memory_space=pltpu.VMEM),) * 2,
        scratch_shapes=[
            vm(KRYLOV + 1, 2, NX, *TILE), vm(2, count, 6, *TILE), vm(count, 4, *TILE), vm(NX, *TILE),
            *halo_scratch(FIELDS, 1), *halo_scratch(2, 2),
            vm(KRYLOV + 1, 16, NZ), vm(128, NZ), vm(3, *TILE), vm(3, 8, *TILE),
            dma((4,)), dma((3, 8)), dma((3, 8)),
        ],
        compiler_params=pltpu.CompilerParams(collective_id=0, has_side_effects=True),
    )(source, sigma_intra, sigma_extra, membrane)


def solution(mesh):
    return jax.shard_map(
        body,
        mesh=mesh,
        in_specs=(
            P(None, "gx", "gy", "gz"),
            P(None, "gx", "gy", "gz"),
            P(None, "gx", "gy", "gz"),
            P("gx", "gy", "gz"),
        ),
        out_specs=(P(None, "gx", "gy", "gz"), P(None, "gx", "gy", "gz")),
        check_vma=False,
    )
```

time: 69.3 us -> 59.6 us (0.86)
  Pallas kernels: 66.4 us -> 56.7 us
    pallas_call x1, Pallas kernels: 66.4 us -> 56.7 us  [body(): pl.pallas_call(functools.partial(cycle_kernel, sizes), out_shape=(out, ou...]
where the time goes in v2:
time: 59.6 us; the launch traced here: 59.3 us
  Pallas kernels  56.7 us (95%)
  local copies, waits for them, and re-layouts  2 us (3%)
  between operations  0.65 us (1%)
    pallas_call x1, Pallas kernels, body(): pl.pallas_call(functools.partial(cycle_kernel, sizes), out_shape=(out, ou...  56.7 us
    unnamed x4, local copies, waits for them, and re-layouts  2 us

profile of v2, /device:TPU:1, one launch (start us, length us, event | category | flops | bytes accessed | tf_op | source)
XLA Modules:
  0.0 59.3 jit_solution(18217008629737412812)
XLA Ops:
  0.6 56.7 %shard_map.59 = (f32[2,4,8,128]{3,2,1,0:T(8,128)}, f32[2,4,8,128]{3,2,1,0:T(8,128)}) custom-call(f32[2,4,8,128]{3,2,1,0:T(8,128)} %source_hbm.1, f32[3,4,8,128]{3,2,1,0:T(8,128)} %intra_hbm.1, f32[3,4,8,128]{3,2,1,0:T(8,128)} %extra_hbm.1, f32[4,8,128]{2,1,0:T(8,128)} %membrane_hbm.1), custom_call_target="tpu_custom_call" | custom-call | tf_op jit(solution)/shard_map/pallas_call | solution.py:473
  57.3 0.0 copy-start
  57.3 1.4 %copy.8 = f32[2,4,8,128]{3,2,1,0:T(8,128)} copy(f32[2,4,8,128]{3,2,1,0:T(8,128)} %get-tuple-element.4) | data formatting | bytes 65536
  58.7 0.0 copy-done
  58.7 0.6 %copy.9 = f32[2,4,8,128]{3,2,1,0:T(8,128)} copy(f32[2,4,8,128]{3,2,1,0:T(8,128)S(1)} %copy-done) | data formatting | bytes 65536
Async XLA Ops:
  57.3 1.4 %copy-start = (f32[2,4,8,128]{3,2,1,0:T(8,128)S(1)}, f32[2,4,8,128]{3,2,1,0:T(8,128)}, u32[]{:S(2)}) copy-start(f32[2,4,8,128]{3,2,1,0:T(8,128)} %get-tuple-element.5) | copy-start | bytes 98308

commit v3 on v2

v3 whole, which is shorter than its diff:
```python
import functools
import itertools

import jax
import jax.numpy as jnp
from jax import lax
from jax.experimental import pallas as pl
from jax.experimental.pallas import tpu as pltpu
from jax.sharding import PartitionSpec as P

KRYLOV = 10
AXES = ("gx", "gy", "gz")
MESH = pl.DeviceIdType.MESH
NX, NY, NZ = 4, 8, 128
TILE = (NY, NZ)
OWN, BESIDE = 0, 1
DIRECTIONS = [
    d for d in itertools.product((-1, 0, 1), repeat=3) if 1 <= sum(abs(a) for a in d) <= 2
]
TILES = (
    [(x, OWN, OWN) for x in range(-1, NX + 1)]
    + [(x, BESIDE, OWN) for x in range(NX)]
    + [(x, OWN, BESIDE) for x in range(NX)]
)
PLACE = {t: n for n, t in enumerate(TILES)}
FIELDS = 7
FACES = [d for d in DIRECTIONS if sum(abs(a) for a in d) == 1]
EDGES = [d for d in DIRECTIONS if sum(abs(a) for a in d) == 2]


class Halo:
    def __init__(self, refs, where, sizes):
        (self.own, self.pack, self.gx, self.gy, self.gz, self.gxy, self.gxz, self.gyz,
         self.send_sem, self.recv_sem) = refs
        self.where, self.sizes, self.count = where, sizes, 0

    def exists(self, direction):
        there = None
        for axis, step in enumerate(direction):
            if step:
                at = self.where[axis]
                ok = at > 0 if step < 0 else at < self.sizes[axis] - 1
                there = ok if there is None else jnp.logical_and(there, ok)
        return there

    def add(self, direction, ends):
        n = self.count
        self.count += 1

        def copy(slot):
            src, dst = ends(slot)
            return pltpu.make_async_remote_copy(
                src_ref=src, dst_ref=dst,
                send_sem=self.send_sem.at[n], recv_sem=self.recv_sem.at[slot, n],
                device_id={AXES[a]: self.where[a] + d for a, d in enumerate(direction) if d},
                device_id_type=MESH,
            )

        return direction, copy

    def planes(self, d, fields, first, count):
        low = NX - first - count if d[0] > 0 else first
        at = 2 - first - count if d[0] > 0 else first
        ghost = 0 if d[0] > 0 else 1
        return self.add(d, lambda slot: (
            self.own.at[fields, pl.ds(low, count)],
            self.gx.at[slot, ghost, fields, pl.ds(at, count)],
        ))

    def rows(self, d, fields, first, count):
        rows = pl.ds(NY - first - count if d[1] > 0 else first, count)
        return self.add(d, lambda slot: (
            self.own.at[fields, :, rows, :], self.gy.at[slot, fields, :, rows, :]
        ))

    def columns(self, d):
        return self.add(d, lambda slot: (self.pack, self.gz.at[slot, 0 if d[2] > 0 else 1]))

    def edge(self, d):
        dx, dy, dz = d
        ghost_x, ghost_z = (0 if dx > 0 else 1), (0 if dz > 0 else 1)
        row = pl.ds(NY - 1 if dy > 0 else 0, 1)
        if dx and dy:
            plane = NX - 1 if dx > 0 else 0
            return self.add(d, lambda slot: (
                self.own.at[:, plane, row, :], self.gxy.at[slot, ghost_x, :, row, :]
            ))
        if dx:
            return self.add(d, lambda slot: (self.pack, self.gxz.at[slot, ghost_x, ghost_z]))
        return self.add(d, lambda slot: (self.pack.at[row, :], self.gyz.at[slot, ghost_z, row, :]))

    def fill_pack(self, values):
        group = lax.broadcasted_iota(jnp.int32, TILE, 1) // 4
        packed = None
        for q, v in enumerate(values):
            moved = pltpu.roll(v, 4 * q + 2, 1)
            packed = moved if packed is None else jnp.where(group == q, moved, packed)
        self.pack[...] = packed

    def start(self, slot, messages):
        for d, copy in messages:
            @pl.when(self.exists(d))
            def _(copy=copy):
                copy(slot).start()

    def sent(self, slot, messages):
        for d, copy in messages:
            @pl.when(self.exists(d))
            def _(copy=copy):
                copy(slot).wait_send()

    def arrived(self, slot, messages):
        for d, copy in messages:
            @pl.when(self.exists(tuple(-a for a in d)))
            def _(copy=copy):
                copy(slot).wait_recv()

    def view(self, slot):
        return View(self, slot)


class View:
    def __init__(self, halo, slot):
        pair = lax.broadcasted_iota(jnp.int32, TILE, 1) % 4 < 2
        self.halo, self.slot, self.made = halo, slot, {}
        self.merge = lambda ref, *at: jnp.where(pair, ref[(slot, *at, 0)], ref[(slot, *at, 1)])
        self.merged = {}

    def columns(self, name, *at):
        if (name, at) not in self.merged:
            self.merged[name, at] = self.merge(getattr(self.halo, name), *at)
        return self.merged[name, at]

    def tile(self, f, x, ty, tz, turn=0):
        key = (f, x, ty, tz, turn)
        if key not in self.made:
            self.made[key] = self.make(f, x, ty, tz, turn)
        return self.made[key]

    def make(self, f, x, ty, tz, turn):
        h = self.halo
        if tz == BESIDE:
            if ty == BESIDE:
                source, plane = self.columns("gyz"), x
            elif x < 0:
                source, plane = self.columns("gxz", 0), NX - 1
            elif x >= NX:
                source, plane = self.columns("gxz", 1), 0
            else:
                source, plane = self.columns("gz"), x
            return pltpu.roll(source, (NZ - (4 * (f * NX + plane) + 2) + turn) % NZ, 1)
        if turn:
            return pltpu.roll(self.tile(f, x, ty, tz), turn % NZ, 1)
        if ty == BESIDE:
            if x < 0:
                return h.gxy[self.slot, 0, f]
            if x >= NX:
                return h.gxy[self.slot, 1, f]
            return h.gy[self.slot, f, x]
        if x < 0:
            return h.gx[self.slot, 0, f, x + 2]
        if x >= NX:
            return h.gx[self.slot, 1, f, x - NX]
        return h.own[f, x]


class Values:
    def __init__(self, values):
        self.values, self.made = values, {}

    def tile(self, f, x, ty, tz, turn=0):
        v = self.values[f][x, ty, tz]
        if not turn:
            return v
        key = (f, x, ty, tz, turn)
        if key not in self.made:
            self.made[key] = pltpu.roll(v, turn % NZ, 1)
        return self.made[key]


def beside(view, f, t, axis, step):
    x, ty, tz = t
    if axis == 0:
        return view.tile(f, x + step, ty, tz)
    if axis == 1:
        edge = lax.broadcasted_iota(jnp.int32, TILE, 0) == (0 if step < 0 else NY - 1)
        shift = 1 if step < 0 else NY - 1
        return jnp.where(
            edge,
            pltpu.roll(view.tile(f, x, 1 - ty, tz), shift, 0),
            pltpu.roll(view.tile(f, x, ty, tz), shift, 0),
        )
    edge = lax.broadcasted_iota(jnp.int32, TILE, 1) == (0 if step < 0 else NZ - 1)
    return jnp.where(edge, view.tile(f, x, ty, 1 - tz, -step), view.tile(f, x, ty, tz, -step))


def two_sum(a, b):
    s = a + b
    t = s - a
    return s, (a - (s - t)) + (b - t)


def add_pair(a, b):
    s, e = two_sum(a[0], b[0])
    return s, e + (a[1] + b[1])


def halves(a):
    c = 4097.0 * a
    top = c - (c - a)
    return top, a - top


def product(a, b, a_halves, b_halves):
    (ah, al), (bh, bl) = a_halves, b_halves
    p = a * b
    return p, ((ah * bh - p) + ah * bl + al * bh) + al * bl


class Pair:
    def __init__(self, high, low):
        self.high, self.low = two_sum(high, low)
        self.halves = halves(self.high)

    def times(self, other):
        p, e = product(self.high, other.high, self.halves, other.halves)
        return p, e + (self.high * other.low + self.low * other.high)


def minimizer(high, low):
    size = KRYLOV + 1
    row = lax.broadcasted_iota(jnp.int32, TILE, 0)
    col = lax.broadcasted_iota(jnp.int32, TILE, 1)
    groups = (NY + 3 - 1, 2)
    assert groups[0] == size - 1

    def column(j, group):
        i = groups[group] - row
        mask = col == lax.shift_right_arithmetic(i * (i + 1), 1) + j
        return tuple(
            jnp.broadcast_to(jnp.sum(jnp.where(mask, v, 0.0), axis=1, keepdims=True), TILE)
            for v in (high, low)
        )

    def place(i):
        return (0, groups[0] - i) if i > groups[1] else (1, groups[1] - i)

    def entry(vectors, i):
        group, r = place(i)
        return tuple(jnp.broadcast_to(v[r : r + 1, :], TILE) for v in vectors[group])

    columns = [{g: column(j, g) for g in range(2) if g == 0 or j <= groups[1]} for j in range(size)]
    first = entry(columns[0], 0)
    right = {0: first, 1: first}
    factors, solved = [], []
    for k in range(size):
        pivot = Pair(*entry(columns[k], k))
        guess = 1.0 / pivot.high
        p, e = product(pivot.high, guess, pivot.halves, halves(guess))
        inverse = Pair(guess, guess * (((1.0 - p) - e) - pivot.low * guess))
        bk = Pair(*entry(right, k))
        solved.append(sum(bk.times(inverse)))
        live = [g for g in range(2) if (g == 0 and k < size - 1) or (g == 1 and k < groups[1])]
        factor = {g: Pair(*Pair(*columns[k][g]).times(inverse)) for g in live}
        factors.append({g: (factor[g].high, factor[g].low) for g in live})
        targets = [(columns[j], Pair(*entry(columns[k], j))) for j in range(k + 1, size)]
        for target, by in targets + [(right, bk)]:
            for g in live:
                if g in target:
                    p, e = factor[g].times(by)
                    s, t = two_sum(target[g][0], -p)
                    target[g] = s, target[g][1] + (t - e)
    z = [None] * size
    for k in range(size - 1, -1, -1):
        rest = solved[k]
        for i in range(size - 1, k, -1):
            rest = rest - entry(factors[k], i)[0] * z[i]
        z[k] = rest
    return z


def cycle_kernel(
    sizes,
    source_hbm, intra_hbm, extra_hbm, membrane_hbm,
    solution_ref, residual_ref, scale_ref,
    basis, coef, block, inverse,
    s_own, s_pack, s_gx, s_gy, s_gz, s_gxy, s_gxz, s_gyz, s_send, s_recv,
    u_own, u_pack, u_gx, u_gy, u_gz, u_gxy, u_gxz, u_gyz, u_send, u_recv,
    gram_rows, gram_all, mine, parts,
    local_sem, sum_send, sum_recv,
):
    where = [lax.axis_index(a) for a in AXES]
    cells = Halo(
        (s_own, s_pack, s_gx, s_gy, s_gz, s_gxy, s_gxz, s_gyz, s_send, s_recv), where, sizes
    )
    halo = Halo(
        (u_own, u_pack, u_gx, u_gy, u_gz, u_gxy, u_gxz, u_gyz, u_send, u_recv), where, sizes
    )

    every = slice(None)
    near, rest, messages = [], [], []
    for d in FACES:
        if d[0]:
            near.append(cells.planes(d, pl.ds(0, 2), 0, 1))
            rest.append(cells.planes(d, pl.ds(2, 5), 0, 1))
            rest.append(cells.planes(d, pl.ds(0, 2), 1, 1))
        elif d[1]:
            near.append(cells.rows(d, pl.ds(2, 2), 0, 1))
            rest.append(cells.rows(d, pl.ds(0, 2), 0, 1))
            rest.append(cells.rows(d, pl.ds(4, 3), 0, 1))
            rest.append(cells.rows(d, pl.ds(2, 2), 1, 1))
        else:
            near.append(cells.columns(d))
    for d in EDGES:
        rest.append(cells.edge(d))
        messages.append(halo.edge(d))
    for d in FACES:
        if d[0]:
            messages.append(halo.planes(d, every, 0, 2))
        elif d[1]:
            messages.append(halo.rows(d, every, 0, 2))
        else:
            messages.append(halo.columns(d))

    loads = [
        pltpu.make_async_copy(ref.at[axis], s_own.at[2 * axis + s], local_sem.at[2 * axis + s])
        for axis in range(3) for s, ref in enumerate((intra_hbm, extra_hbm))
    ] + [
        pltpu.make_async_copy(membrane_hbm, s_own.at[6], local_sem.at[6]),
        pltpu.make_async_copy(source_hbm, basis.at[0], local_sem.at[7]),
    ]
    for c in loads:
        c.start()
    for h in (cells, halo):
        for ref in (h.gx, h.gy, h.gz, h.gxy, h.gxz, h.gyz):
            ref[...] = jnp.zeros_like(ref)

    barrier = pltpu.get_barrier_semaphore()
    expected = 0
    for d in DIRECTIONS:
        there = cells.exists(d)
        expected = expected + jnp.where(there, 1, 0)

        @pl.when(there)
        def _(d=d):
            pl.semaphore_signal(
                barrier, inc=1,
                device_id={AXES[a]: where[a] + step for a, step in enumerate(d) if step},
                device_id_type=MESH,
            )
    gram_all[...] = jnp.zeros_like(gram_all)
    for k in range(1, KRYLOV + 1):
        basis[k] = jnp.zeros_like(basis.at[k])
    for c in loads:
        c.wait()
    cells.fill_pack([s_own[f, x] for f in range(FIELDS) for x in range(NX)])
    pl.semaphore_wait(barrier, expected)

    cells.start(0, near)
    cells.start(0, rest)

    def coefficients(view, beside, tiles):
        for t in tiles:
            n = PLACE[t]
            diagonals = []
            for s in range(2):
                total = None
                for axis in range(3):
                    here = view.tile(2 * axis + s, *t)
                    lower = 0.5 * (here + beside(view, 2 * axis + s, t, axis, -1))
                    upper = 0.5 * (here + beside(view, 2 * axis + s, t, axis, 1))
                    coef[s, n, 2 * axis] = lower
                    coef[s, n, 2 * axis + 1] = upper
                    total = upper + lower if total is None else total + upper + lower
                diagonals.append(total)
            di, de, m = diagonals[0], diagonals[1], view.tile(6, *t)
            det = m * di + m * de + di * de
            inside = m > 0.0
            over = jnp.where(inside, 1.0 / jnp.where(inside, det, 1.0), 0.0)
            block[n, 0] = de * over
            block[n, 1] = m * over
            block[n, 2] = -di * over
            block[n, 3] = (m + di) * over
            if t in own:
                inverse[t[0]] = (di + de) * over

    def beside_own(view, f, t, axis, step):
        if axis != 1:
            return beside(view, f, t, axis, step)
        row = NY - 1 if step < 0 else 0
        edge = lax.broadcasted_iota(jnp.int32, TILE, 0) == NY - 1 - row
        ghost = s_gy[0, f, t[0], pl.ds(row, 1), :]
        return jnp.where(edge, ghost, pltpu.roll(view.tile(f, *t), 1 if step < 0 else NY - 1, 0))

    own = [(x, OWN, OWN) for x in range(NX)]
    def solved(t, a, b):
        n = PLACE[t]
        return block[n, 0] * a + block[n, 1] * b, block[n, 2] * a + block[n, 3] * b

    def apply(view, t):
        n = PLACE[t]
        off = []
        for s in range(2):
            total = None
            for axis in range(3):
                for side, step in enumerate((-1, 1)):
                    term = coef[s, n, 2 * axis + side] * beside(view, s, t, axis, step)
                    total = term if total is None else total + term
            off.append(total)
        return off[0], off[0] + off[1]

    def load(k):
        return [[basis[k, s, x] for x in range(NX)] for s in range(2)]

    def keep(k, v):
        for s in range(2):
            for x in range(NX):
                basis[k, s, x] = v[s][x]

    def stage(v):
        values = [[None] * NX for _ in range(2)]
        for x in range(NX):
            values[0][x], values[1][x] = solved(own[x], v[0][x], v[1][x])
        for s in range(2):
            for x in range(NX):
                u_own[s, x] = values[s][x]
        halo.fill_pack(values[0] + values[1])

    def gram_row(k):
        at = load(k)
        for i in range(KRYLOV + 1):
            total = None
            for s in range(2):
                for x in range(NX):
                    term = at[s][x] * basis[i, s, x]
                    total = term if total is None else total + term
            gram_rows[k, pl.ds(i, 1), :] = jnp.sum(total, axis=0, keepdims=True)

    def two_steps(slot):
        view = halo.view(slot)
        first, next_u = {}, [{}, {}]
        for t in TILES:
            first[t] = apply(view, t)
            next_u[0][t], next_u[1][t] = solved(t, *first[t])
        values = Values(next_u)
        second = [apply(values, t) for t in own]
        return (
            [[first[t][s] for t in own] for s in range(2)],
            [[second[x][s] for x in range(NX)] for s in range(2)],
        )

    def combine(f, *vs):
        return [[f(*(v[s][x] for v in vs)) for x in range(NX)] for s in range(2)]

    def advance(k, slot):
        w, b = two_steps(slot)
        odd = combine(lambda p, q: 2.0 * p - q, w, load(k - 1))
        even = combine(lambda p, q, r: 4.0 * p - 2.0 * q - r, b, load(k), load(k - 2))
        return odd, even

    cells.arrived(0, near)
    coefficients(cells.view(0), beside_own, own)
    stage(load(0))
    halo.start(0, messages)
    gram_row(0)
    cells.sent(0, near + rest)
    cells.arrived(0, rest)
    coefficients(cells.view(0), beside, [t for t in TILES if t not in own])
    halo.sent(0, messages)
    halo.arrived(0, messages)
    odd, b = two_steps(0)
    even = combine(lambda p, q: 2.0 * p - q, b, load(0))
    stage(even)
    halo.start(1, messages)
    keep(1, odd)
    keep(2, even)

    def step(r, carry):
        k, slot = 2 * r, lax.rem(r, 2)
        gram_row(k - 1)
        gram_row(k)
        halo.sent(slot, messages)
        halo.arrived(slot, messages)
        odd, even = advance(k, slot)
        stage(even)
        halo.start(1 - slot, messages)
        keep(k + 1, odd)
        keep(k + 2, even)
        return carry

    rounds = KRYLOV // 2
    lax.fori_loop(1, rounds - 1, step, 0)
    gram_row(KRYLOV - 3)
    gram_row(KRYLOV - 2)
    last = (rounds - 1) % 2
    halo.sent(last, messages)
    halo.arrived(last, messages)
    odd, even = advance(KRYLOV - 2, last)
    keep(KRYLOV - 1, odd)
    keep(KRYLOV, even)
    gram_row(KRYLOV - 1)
    gram_row(KRYLOV)

    at = 0
    for k in range(KRYLOV + 1):
        gram_all[pl.ds(at, k + 1), :] = gram_rows[k, pl.ds(0, k + 1), :]
        at += k + 1
    ones = jnp.ones(TILE, jnp.bfloat16)
    left, totals = gram_all[...], []
    for _ in range(3):
        piece = left.astype(jnp.bfloat16)
        left = left - piece.astype(jnp.float32)
        totals.append(lax.dot_general(
            ones, piece, (((1,), (1,)), ((), ())), preferred_element_type=jnp.float32
        )[0:1, :])
    high, low = two_sum(totals[0], totals[1])
    low = low + totals[2]
    for n, d in enumerate((2, 1, 0)):
        size = sizes[d]
        mine[n, 0:1, :] = high
        mine[n, 1:2, :] = low
        parts[n, where[d], 0:1, :] = high
        parts[n, where[d], 1:2, :] = low

        def copy(j, slot, other):
            return pltpu.make_async_remote_copy(
                src_ref=mine.at[n, pl.ds(0, 2), :], dst_ref=parts.at[n, slot, pl.ds(0, 2), :],
                send_sem=sum_send.at[n, j], recv_sem=sum_recv.at[n, slot],
                device_id={AXES[d]: other}, device_id_type=MESH,
            )

        others = [(j, lax.rem(where[d] + j, size)) for j in range(1, size)]
        for j, other in others:
            copy(j, where[d], other).start()
        for j, other in others:
            copy(j, other, other).wait_recv()
        for j, other in others:
            copy(j, where[d], other).wait_send()
        terms = [(parts[n, j, 0:1, :], parts[n, j, 1:2, :]) for j in range(size)]
        while len(terms) > 1:
            terms = [add_pair(terms[i], terms[i + 1]) for i in range(0, len(terms), 2)]
        high, low = two_sum(*terms[0])

    z = minimizer(jnp.broadcast_to(high, TILE), jnp.broadcast_to(low, TILE))
    size = KRYLOV + 1
    total = z[0]
    for k in range(1, size):
        total = total + z[k]
    scale_ref[...] = 1.0 / total
    rho = z
    slope = [None] * size
    running = jnp.zeros(TILE, jnp.float32)
    weighted = jnp.zeros(TILE, jnp.float32)
    for j in range(KRYLOV - 1, -1, -1):
        running = running + rho[j + 1]
        weighted = weighted + running
        slope[j] = weighted
    coeffs = [slope[0]] + [2.0 * slope[j] for j in range(1, KRYLOV)]

    for x in range(NX):
        combined = []
        for s in range(2):
            vectors = [basis[k, s, x] for k in range(size)]
            r = rho[0] * vectors[0]
            c = coeffs[0] * vectors[0]
            for k in range(1, size):
                r = r + rho[k] * vectors[k]
                if k < KRYLOV:
                    c = c + coeffs[k] * vectors[k]
            residual_ref[s, x] = r
            combined.append(c)
        n = PLACE[own[x]]
        solution_ref[0, x] = inverse[x] * combined[0] + block[n, 2] * combined[1]
        solution_ref[1, x] = block[n, 2] * combined[0] + block[n, 3] * combined[1]


def halo_scratch(fields, slots, count):
    vm = lambda *s: pltpu.VMEM(s, jnp.float32)
    dma = pltpu.SemaphoreType.DMA
    return [
        vm(fields, NX, *TILE), vm(*TILE),
        vm(slots, 2, fields, 2, *TILE), vm(slots, fields, NX, *TILE), vm(slots, 2, *TILE),
        vm(slots, 2, fields, *TILE), vm(slots, 2, 2, *TILE), vm(slots, 2, *TILE),
        dma((count,)), dma((slots, count)),
    ]


def body(source, sigma_intra, sigma_extra, membrane):
    sizes = tuple(lax.axis_size(a) for a in AXES)
    f32 = jnp.float32
    vm = lambda *s: pltpu.VMEM(s, f32)
    dma = pltpu.SemaphoreType.DMA
    count = len(TILES)
    unscaled, remainder, scale = pl.pallas_call(
        functools.partial(cycle_kernel, sizes),
        out_shape=(vm(*source.shape), vm(*source.shape), vm(*TILE)),
        in_specs=[pl.BlockSpec(memory_space=pl.ANY)] * 4,
        out_specs=(pl.BlockSpec(memory_space=pltpu.VMEM),) * 3,
        scratch_shapes=[
            vm(KRYLOV + 1, 2, NX, *TILE), vm(2, count, 6, *TILE), vm(count, 4, *TILE), vm(NX, *TILE),
            *halo_scratch(FIELDS, 1, 28), *halo_scratch(2, 2, len(DIRECTIONS)),
            vm(KRYLOV + 1, 16, NZ), vm(128, NZ), vm(3, *TILE), vm(3, 8, *TILE),
            dma((8,)), dma((3, 8)), dma((3, 8)),
        ],
        compiler_params=pltpu.CompilerParams(collective_id=0, has_side_effects=True),
    )(source, sigma_intra, sigma_extra, membrane)
    return unscaled * scale, remainder * scale


def solution(mesh):
    return jax.shard_map(
        body,
        mesh=mesh,
        in_specs=(
            P(None, "gx", "gy", "gz"),
            P(None, "gx", "gy", "gz"),
            P(None, "gx", "gy", "gz"),
            P("gx", "gy", "gz"),
        ),
        out_specs=(P(None, "gx", "gy", "gz"), P(None, "gx", "gy", "gz")),
        check_vma=False,
    )
```

time: 59.6 us -> 55.6 us (0.933)
  Pallas kernels: 56.7 us -> 54.1 us
  local copies, waits for them, and re-layouts: 2 us -> 0 us
  other arithmetic: 0 us -> 0.63 us
    pallas_call x1, Pallas kernels: 56.7 us -> 54.1 us  [body(): pl.pallas_call(functools.partial(cycle_kernel, sizes), out_shape=(vm(*sou...]
    unnamed x4 -> x0, local copies, waits for them, and re-layouts: 2 us -> none
    mul x0 -> x1, other arithmetic: none -> 0.63 us  [body(): return (unscaled * scale, remainder * scale)]
where the time goes in v3:
time: 55.6 us; the launch traced here: 55.4 us
  Pallas kernels  54.1 us (97%)
  between operations  0.64 us (1%)
  other arithmetic  0.63 us (1%)
    pallas_call x1, Pallas kernels, body(): pl.pallas_call(functools.partial(cycle_kernel, sizes), out_shape=(vm(*sou...  54.1 us

profile of v3, /device:TPU:1, one launch (start us, length us, event | category | flops | bytes accessed | tf_op | source)
XLA Modules:
  0.0 55.4 jit_solution(17728701551619528445)
XLA Ops:
  0.6 54.1 %shard_map.59 = (f32[2,4,8,128]{3,2,1,0:T(8,128)S(1)}, f32[2,4,8,128]{3,2,1,0:T(8,128)S(1)}, f32[8,128]{1,0:T(8,128)S(1)}) custom-call(f32[2,4,8,128]{3,2,1,0:T(8,128)} %source_hbm.1, f32[3,4,8,128]{3,2,1,0:T(8,128)} %intra_hbm.1, f32[3,4,8,128]{3,2,1,0:T(8,128)} %extra_hbm.1, f32[4,8,128]{2,1,0:T(8,128)} %membrane_hbm.1), custom_call_target="tpu_custom_call" | custom-call | tf_op jit(solution)/shard_map/pallas_call | solution.py:594
  54.7 0.6 %broadcast_multiply_fusion = (f32[2,4,8,128]{3,2,1,0:T(8,128)}, f32[2,4,8,128]{3,2,1,0:T(8,128)}) fusion(f32[2,4,8,128]{3,2,1,0:T(8,128)S(1)} %get-tuple-element.7, f32[8,128]{1,0:T(8,128)S(1)} %get-tuple-element.6, f32[2,4,8,128]{3,2,1,0:T(8,128)S(1)} %get-tuple-element.5), kind=kLoop, calls=%fused_computation | loop fusion | flops 16384 | bytes 135168 | tf_op jit(solution)/shard_map/mul | solution.py:607

commit v4 on v3

--- a/solution.py
+++ b/solution.py
@@ -14,24 +14,39 @@
 NX, NY, NZ = 4, 8, 128
 TILE = (NY, NZ)
 OWN, BESIDE = 0, 1
-DIRECTIONS = [
-    d for d in itertools.product((-1, 0, 1), repeat=3) if 1 <= sum(abs(a) for a in d) <= 2
-]
-TILES = (
-    [(x, OWN, OWN) for x in range(-1, NX + 1)]
-    + [(x, BESIDE, OWN) for x in range(NX)]
-    + [(x, OWN, BESIDE) for x in range(NX)]
+FACES, EDGES, CORNERS = (
+    [d for d in itertools.product((-1, 0, 1), repeat=3) if sum(abs(a) for a in d) == n]
+    for n in (1, 2, 3)
 )
+DIRECTIONS = FACES + EDGES + CORNERS
+FIELDS = 7
+SHALLOW, DEEP = 2, 4
+
+
+def tiles(reach):
+    return [
+        (x, ty, tz)
+        for ty in (OWN, BESIDE) for tz in (OWN, BESIDE) for x in range(-reach, NX + reach)
+        if max(-x, x - NX + 1, 0) + ty + tz <= reach
+    ]
+
+
+TILES = tiles(DEEP - 1)
 PLACE = {t: n for n, t in enumerate(TILES)}
-FIELDS = 7
-FACES = [d for d in DIRECTIONS if sum(abs(a) for a in d) == 1]
-EDGES = [d for d in DIRECTIONS if sum(abs(a) for a in d) == 2]
+
+
+def toward(where, sizes, direction):
+    return {
+        AXES[a]: lax.rem(where[a] + step + sizes[a], sizes[a])
+        for a, step in enumerate(direction) if step
+    }
 
 
 class Halo:
-    def __init__(self, refs, where, sizes):
-        (self.own, self.pack, self.gx, self.gy, self.gz, self.gxy, self.gxz, self.gyz,
+    def __init__(self, depth, refs, where, sizes):
+        (self.own, self.pack, self.gx, self.gy, self.gz, self.gxy, self.gxz, self.gyz, self.gxyz,
          self.send_sem, self.recv_sem) = refs
+        self.depth, self.stride, self.each = depth, 2 * depth, NZ // (2 * depth)
         self.where, self.sizes, self.count = where, sizes, 0
 
     def exists(self, direction):
@@ -52,7 +67,7 @@
             return pltpu.make_async_remote_copy(
                 src_ref=src, dst_ref=dst,
                 send_sem=self.send_sem.at[n], recv_sem=self.recv_sem.at[slot, n],
-                device_id={AXES[a]: self.where[a] + d for a, d in enumerate(direction) if d},
+                device_id=toward(self.where, self.sizes, direction),
                 device_id_type=MESH,
             )
 
@@ -60,7 +75,7 @@
 
     def planes(self, d, fields, first, count):
         low = NX - first - count if d[0] > 0 else first
-        at = 2 - first - count if d[0] > 0 else first
+        at = self.depth - first - count if d[0] > 0 else first
         ghost = 0 if d[0] > 0 else 1
         return self.add(d, lambda slot: (
             self.own.at[fields, pl.ds(low, count)],
@@ -79,23 +94,31 @@
     def edge(self, d):
         dx, dy, dz = d
         ghost_x, ghost_z = (0 if dx > 0 else 1), (0 if dz > 0 else 1)
-        row = pl.ds(NY - 1 if dy > 0 else 0, 1)
-        if dx and dy:
-            plane = NX - 1 if dx > 0 else 0
+        count = self.depth - sum(abs(a) for a in d) + 1
+        row = pl.ds(NY - count if dy > 0 else 0, count)
+        if not dz:
+            planes = pl.ds(NX - count if dx > 0 else 0, count)
             return self.add(d, lambda slot: (
-                self.own.at[:, plane, row, :], self.gxy.at[slot, ghost_x, :, row, :]
+                self.own.at[:, planes, row, :], self.gxy.at[slot, ghost_x, :, :, row, :]
             ))
-        if dx:
+        if not dy:
             return self.add(d, lambda slot: (self.pack, self.gxz.at[slot, ghost_x, ghost_z]))
-        return self.add(d, lambda slot: (self.pack.at[row, :], self.gyz.at[slot, ghost_z, row, :]))
+        if not dx:
+            return self.add(d, lambda slot: (
+                self.pack.at[:, row, :], self.gyz.at[slot, ghost_z, :, row, :]
+            ))
+        return self.add(d, lambda slot: (
+            self.pack.at[:, row, :], self.gxyz.at[slot, ghost_x, ghost_z, :, row, :]
+        ))
 
     def fill_pack(self, values):
-        group = lax.broadcasted_iota(jnp.int32, TILE, 1) // 4
-        packed = None
-        for q, v in enumerate(values):
-            moved = pltpu.roll(v, 4 * q + 2, 1)
-            packed = moved if packed is None else jnp.where(group == q, moved, packed)
-        self.pack[...] = packed
+        group = lax.broadcasted_iota(jnp.int32, TILE, 1) // self.stride
+        for first in range(0, len(values), self.each):
+            packed = None
+            for q, v in enumerate(values[first : first + self.each]):
+                moved = pltpu.roll(v, self.stride * q + self.depth, 1)
+                packed = moved if packed is None else jnp.where(group == q, moved, packed)
+            self.pack[first // self.each] = packed
 
     def start(self, slot, messages):
         for d, copy in messages:
@@ -121,14 +144,16 @@
 
 class View:
     def __init__(self, halo, slot):
-        pair = lax.broadcasted_iota(jnp.int32, TILE, 1) % 4 < 2
-        self.halo, self.slot, self.made = halo, slot, {}
-        self.merge = lambda ref, *at: jnp.where(pair, ref[(slot, *at, 0)], ref[(slot, *at, 1)])
-        self.merged = {}
+        self.halo, self.slot, self.made, self.merged = halo, slot, {}, {}
 
     def columns(self, name, *at):
         if (name, at) not in self.merged:
-            self.merged[name, at] = self.merge(getattr(self.halo, name), *at)
+            h, (*before, pack) = self.halo, at
+            ref = getattr(h, name)
+            low = lax.broadcasted_iota(jnp.int32, TILE, 1) % h.stride < h.depth
+            self.merged[name, at] = jnp.where(
+                low, ref[(self.slot, *before, 0, pack)], ref[(self.slot, *before, 1, pack)]
+            )
         return self.merged[name, at]
 
     def tile(self, f, x, ty, tz, turn=0):
@@ -139,29 +164,21 @@
 
     def make(self, f, x, ty, tz, turn):
         h = self.halo
+        outside = (0,) if x < 0 else (1,) if x >= NX else ()
         if tz == BESIDE:
-            if ty == BESIDE:
-                source, plane = self.columns("gyz"), x
-            elif x < 0:
-                source, plane = self.columns("gxz", 0), NX - 1
-            elif x >= NX:
-                source, plane = self.columns("gxz", 1), 0
-            else:
-                source, plane = self.columns("gz"), x
-            return pltpu.roll(source, (NZ - (4 * (f * NX + plane) + 2) + turn) % NZ, 1)
+            pack, q = divmod(f * NX + x % NX, h.each)
+            name = "g" + ("x" if outside else "") + ("y" if ty == BESIDE else "") + "z"
+            source = self.columns(name, *outside, pack)
+            return pltpu.roll(source, (turn - h.stride * q - h.depth) % NZ, 1)
         if turn:
             return pltpu.roll(self.tile(f, x, ty, tz), turn % NZ, 1)
         if ty == BESIDE:
-            if x < 0:
-                return h.gxy[self.slot, 0, f]
-            if x >= NX:
-                return h.gxy[self.slot, 1, f]
-            return h.gy[self.slot, f, x]
-        if x < 0:
-            return h.gx[self.slot, 0, f, x + 2]
-        if x >= NX:
-            return h.gx[self.slot, 1, f, x - NX]
-        return h.own[f, x]
+            if not outside:
+                return h.gy[self.slot, f, x]
+            return h.gxy[self.slot, outside[0], f, x + h.depth - 1 if x < 0 else x - NX]
+        if not outside:
+            return h.own[f, x]
+        return h.gx[self.slot, outside[0], f, x + h.depth if x < 0 else x - NX]
 
 
 class Values:
@@ -284,17 +301,14 @@
     source_hbm, intra_hbm, extra_hbm, membrane_hbm,
     solution_ref, residual_ref, scale_ref,
     basis, coef, block, inverse,
-    s_own, s_pack, s_gx, s_gy, s_gz, s_gxy, s_gxz, s_gyz, s_send, s_recv,
-    u_own, u_pack, u_gx, u_gy, u_gz, u_gxy, u_gxz, u_gyz, u_send, u_recv,
-    gram_rows, gram_all, mine, parts,
-    local_sem, sum_send, sum_recv,
+    s_own, u_own, *refs,
 ):
+    groups = [refs[10 * n : 10 * n + 10] for n in range(4)]
+    gram_rows, gram_all, mine, parts, local_sem, sum_send, sum_recv = refs[40:]
     where = [lax.axis_index(a) for a in AXES]
-    cells = Halo(
-        (s_own, s_pack, s_gx, s_gy, s_gz, s_gxy, s_gxz, s_gyz, s_send, s_recv), where, sizes
-    )
-    halo = Halo(
-        (u_own, u_pack, u_gx, u_gy, u_gz, u_gxy, u_gxz, u_gyz, u_send, u_recv), where, sizes
+    cells, deep_cells, halo, deep_halo = (
+        Halo(depth, (own, *group), where, sizes)
+        for depth, own, group in zip((SHALLOW, DEEP) * 2, (s_own, s_own, u_own, u_own), groups)
     )
 
     every = slice(None)
@@ -313,14 +327,24 @@
             near.append(cells.columns(d))
     for d in EDGES:
         rest.append(cells.edge(d))
-        messages.append(halo.edge(d))
-    for d in FACES:
-        if d[0]:
-            messages.append(halo.planes(d, every, 0, 2))
-        elif d[1]:
-            messages.append(halo.rows(d, every, 0, 2))
-        else:
-            messages.append(halo.columns(d))
+
+    def all_messages(h, trim):
+        made = [h.edge(d) for d in (CORNERS if h.depth > 2 else []) + EDGES]
+        for d in FACES:
+            if d[0] and trim:
+                made.append(h.planes(d, pl.ds(0, 2), 0, h.depth))
+                made.append(h.planes(d, pl.ds(2, 5), 0, h.depth - 1))
+            elif d[0]:
+                made.append(h.planes(d, every, 0, h.depth))
+            elif d[1]:
+                made.append(h.rows(d, every, 0, h.depth))
+            else:
+                made.append(h.columns(d))
+        return made
+
+    messages = all_messages(halo, False)
+    deep_rest = all_messages(deep_cells, True)
+    deep_messages = all_messages(deep_halo, False)
 
     loads = [
         pltpu.make_async_copy(ref.at[axis], s_own.at[2 * axis + s], local_sem.at[2 * axis + s])
@@ -331,8 +355,8 @@
     ]
     for c in loads:
         c.start()
-    for h in (cells, halo):
-        for ref in (h.gx, h.gy, h.gz, h.gxy, h.gxz, h.gyz):
+    for h in (cells, deep_cells, halo, deep_halo):
+        for ref in (h.gx, h.gy, h.gz, h.gxy, h.gxz, h.gyz, h.gxyz):
             ref[...] = jnp.zeros_like(ref)
 
     barrier = pltpu.get_barrier_semaphore()
@@ -345,9 +369,20 @@
         def _(d=d):
             pl.semaphore_signal(
                 barrier, inc=1,
-                device_id={AXES[a]: where[a] + step for a, step in enumerate(d) if step},
+                device_id=toward(where, sizes, d),
                 device_id_type=MESH,
             )
+    for d in range(3):
+        for far in range(6, sizes[d]):
+            for step in (-far, far):
+                there = where[d] >= far if step < 0 else where[d] < sizes[d] - far
+                expected = expected + jnp.where(there, 1, 0)
+
+                @pl.when(there)
+                def _(d=d, step=step):
+                    pl.semaphore_signal(
+                        barrier, inc=1, device_id={AXES[d]: lax.rem(where[d] + step + sizes[d], sizes[d])}, device_id_type=MESH
+                    )
     gram_all[...] = jnp.zeros_like(gram_all)
     for k in range(1, KRYLOV + 1):
         basis[k] = jnp.zeros_like(basis.at[k])
@@ -389,7 +424,7 @@
             return beside(view, f, t, axis, step)
         row = NY - 1 if step < 0 else 0
         edge = lax.broadcasted_iota(jnp.int32, TILE, 0) == NY - 1 - row
-        ghost = s_gy[0, f, t[0], pl.ds(row, 1), :]
+        ghost = cells.gy[0, f, t[0], pl.ds(row, 1), :]
         return jnp.where(edge, ghost, pltpu.roll(view.tile(f, *t), 1 if step < 0 else NY - 1, 0))
 
     own = [(x, OWN, OWN) for x in range(NX)]
@@ -417,14 +452,14 @@
             for x in range(NX):
                 basis[k, s, x] = v[s][x]
 
-    def stage(v):
+    def stage(h, v):
         values = [[None] * NX for _ in range(2)]
         for x in range(NX):
             values[0][x], values[1][x] = solved(own[x], v[0][x], v[1][x])
         for s in range(2):
             for x in range(NX):
                 u_own[s, x] = values[s][x]
-        halo.fill_pack(values[0] + values[1])
+        h.fill_pack(values[0] + values[1])
 
     def gram_row(k):
         at = load(k)
@@ -436,70 +471,68 @@
                     total = term if total is None else total + term
             gram_rows[k, pl.ds(i, 1), :] = jnp.sum(total, axis=0, keepdims=True)
 
-    def two_steps(slot):
-        view = halo.view(slot)
-        first, next_u = {}, [{}, {}]
-        for t in TILES:
-            first[t] = apply(view, t)
-            next_u[0][t], next_u[1][t] = solved(t, *first[t])
-        values = Values(next_u)
-        second = [apply(values, t) for t in own]
-        return (
-            [[first[t][s] for t in own] for s in range(2)],
-            [[second[x][s] for x in range(NX)] for s in range(2)],
-        )
+    def powers(h, slot):
+        view, made = h.view(slot), []
+        for reach in range(h.depth - 1, -1, -1):
+            now = {t: apply(view, t) for t in tiles(reach)}
+            made.append([[now[t][s] for t in own] for s in range(2)])
+            if reach:
+                then = {t: solved(t, *now[t]) for t in now}
+                view = Values([{t: then[t][s] for t in then} for s in range(2)])
+        return made
 
     def combine(f, *vs):
         return [[f(*(v[s][x] for v in vs)) for x in range(NX)] for s in range(2)]
 
-    def advance(k, slot):
-        w, b = two_steps(slot)
-        odd = combine(lambda p, q: 2.0 * p - q, w, load(k - 1))
-        even = combine(lambda p, q, r: 4.0 * p - 2.0 * q - r, b, load(k), load(k - 2))
-        return odd, even
+    def advance(k, h, slot):
+        here = load(k)
+        made = powers(h, slot)
+        terms = [
+            made[0],
+            combine(lambda b, a: 2.0 * b - a, made[1], here),
+        ]
+        if h.depth > 2:
+            terms.append(combine(lambda b, a: 4.0 * b - 3.0 * a, made[2], made[0]))
+            terms.append(combine(lambda b, a, r: 8.0 * b - 8.0 * a + r, made[3], made[1], here))
+        if k == 0:
+            return terms
+        return [combine(lambda t, p: 2.0 * t - p, t, load(abs(k - 1 - j))) for j, t in enumerate(terms)]
 
     cells.arrived(0, near)
     coefficients(cells.view(0), beside_own, own)
-    stage(load(0))
+    stage(halo, load(0))
     halo.start(0, messages)
+    deep_cells.fill_pack([s_own[f, x] for f in range(FIELDS) for x in range(NX)])
+    deep_cells.start(0, deep_rest)
     gram_row(0)
     cells.sent(0, near + rest)
     cells.arrived(0, rest)
-    coefficients(cells.view(0), beside, [t for t in TILES if t not in own])
+    coefficients(cells.view(0), beside, [t for t in tiles(SHALLOW - 1) if t not in own])
     halo.sent(0, messages)
     halo.arrived(0, messages)
-    odd, b = two_steps(0)
-    even = combine(lambda p, q: 2.0 * p - q, b, load(0))
-    stage(even)
-    halo.start(1, messages)
-    keep(1, odd)
-    keep(2, even)
-
-    def step(r, carry):
-        k, slot = 2 * r, lax.rem(r, 2)
-        gram_row(k - 1)
-        gram_row(k)
-        halo.sent(slot, messages)
-        halo.arrived(slot, messages)
-        odd, even = advance(k, slot)
-        stage(even)
-        halo.start(1 - slot, messages)
-        keep(k + 1, odd)
-        keep(k + 2, even)
-        return carry
-
-    rounds = KRYLOV // 2
-    lax.fori_loop(1, rounds - 1, step, 0)
-    gram_row(KRYLOV - 3)
-    gram_row(KRYLOV - 2)
-    last = (rounds - 1) % 2
-    halo.sent(last, messages)
-    halo.arrived(last, messages)
-    odd, even = advance(KRYLOV - 2, last)
-    keep(KRYLOV - 1, odd)
-    keep(KRYLOV, even)
-    gram_row(KRYLOV - 1)
-    gram_row(KRYLOV)
+    made = advance(0, halo, 0)
+    stage(deep_halo, made[-1])
+    deep_halo.start(0, deep_messages)
+    keep(1, made[0])
+    keep(2, made[1])
+    gram_row(1)
+    gram_row(2)
+    deep_cells.sent(0, deep_rest)
+    deep_cells.arrived(0, deep_rest)
+    coefficients(deep_cells.view(0), beside, [
+        t for t in TILES if t[1] == BESIDE or t[2] == BESIDE or t not in tiles(SHALLOW - 1)
+    ])
+    for slot, k in enumerate((2, 6)):
+        deep_halo.sent(slot, deep_messages)
+        deep_halo.arrived(slot, deep_messages)
+        made = advance(k, deep_halo, slot)
+        if slot == 0:
+            stage(deep_halo, made[-1])
+            deep_halo.start(1, deep_messages)
+        for j, v in enumerate(made):
+            keep(k + 1 + j, v)
+        for j in range(len(made)):
+            gram_row(k + 1 + j)
 
     at = 0
     for k in range(KRYLOV + 1):
@@ -574,13 +607,15 @@
         solution_ref[1, x] = block[n, 2] * combined[0] + block[n, 3] * combined[1]
 
 
-def halo_scratch(fields, slots, count):
+def halo_scratch(depth, fields, slots, count):
     vm = lambda *s: pltpu.VMEM(s, jnp.float32)
     dma = pltpu.SemaphoreType.DMA
+    packs = -(-fields * NX // (NZ // (2 * depth)))
     return [
-        vm(fields, NX, *TILE), vm(*TILE),
-        vm(slots, 2, fields, 2, *TILE), vm(slots, fields, NX, *TILE), vm(slots, 2, *TILE),
-        vm(slots, 2, fields, *TILE), vm(slots, 2, 2, *TILE), vm(slots, 2, *TILE),
+        vm(packs, *TILE),
+        vm(slots, 2, fields, depth, *TILE), vm(slots, fields, NX, *TILE),
+        vm(slots, 2, packs, *TILE), vm(slots, 2, fields, depth - 1, *TILE),
+        vm(slots, 2, 2, packs, *TILE), vm(slots, 2, packs, *TILE), vm(slots, 2, 2, packs, *TILE),
         dma((count,)), dma((slots, count)),
     ]
 
@@ -598,7 +633,9 @@
         out_specs=(pl.BlockSpec(memory_space=pltpu.VMEM),) * 3,
         scratch_shapes=[
             vm(KRYLOV + 1, 2, NX, *TILE), vm(2, count, 6, *TILE), vm(count, 4, *TILE), vm(NX, *TILE),
-            *halo_scratch(FIELDS, 1, 28), *halo_scratch(2, 2, len(DIRECTIONS)),
+            vm(FIELDS, NX, *TILE), vm(2, NX, *TILE),
+            *halo_scratch(SHALLOW, FIELDS, 1, 28), *halo_scratch(DEEP, FIELDS, 1, 28),
+            *halo_scratch(SHALLOW, 2, 1, 18), *halo_scratch(DEEP, 2, 2, 26),
             vm(KRYLOV + 1, 16, NZ), vm(128, NZ), vm(3, *TILE), vm(3, 8, *TILE),
             dma((8,)), dma((3, 8)), dma((3, 8)),
         ],

time: 55.6 us -> 49.1 us (0.88)
  Pallas kernels: 54.1 us -> 47.6 us
    pallas_call x1, Pallas kernels: 54.1 us -> 47.6 us  [body(): pl.pallas_call(functools.partial(cycle_kernel, sizes), out_shape=(vm(*sou...]
where the time goes in v4:
time: 49.1 us; the launch traced here: 48.9 us
  Pallas kernels  47.6 us (97%)
  between operations  0.64 us (1%)
  other arithmetic  0.63 us (1%)
    pallas_call x1, Pallas kernels, body(): pl.pallas_call(functools.partial(cycle_kernel, sizes), out_shape=(vm(*sou...  47.6 us

profile of v4, /device:TPU:1, one launch (start us, length us, event | category | flops | bytes accessed | tf_op | source)
XLA Modules:
  0.0 48.9 jit_solution(7486191436588733735)
XLA Ops:
  0.6 47.6 %shard_map.59 = (f32[2,4,8,128]{3,2,1,0:T(8,128)S(1)}, f32[2,4,8,128]{3,2,1,0:T(8,128)S(1)}, f32[8,128]{1,0:T(8,128)S(1)}) custom-call(f32[2,4,8,128]{3,2,1,0:T(8,128)} %source_hbm.1, f32[3,4,8,128]{3,2,1,0:T(8,128)} %intra_hbm.1, f32[3,4,8,128]{3,2,1,0:T(8,128)} %extra_hbm.1, f32[4,8,128]{2,1,0:T(8,128)} %membrane_hbm.1), custom_call_target="tpu_custom_call" | custom-call | tf_op jit(solution)/shard_map/pallas_call | solution.py:629
  48.3 0.6 %broadcast_multiply_fusion = (f32[2,4,8,128]{3,2,1,0:T(8,128)}, f32[2,4,8,128]{3,2,1,0:T(8,128)}) fusion(f32[2,4,8,128]{3,2,1,0:T(8,128)S(1)} %get-tuple-element.7, f32[8,128]{1,0:T(8,128)S(1)} %get-tuple-element.6, f32[2,4,8,128]{3,2,1,0:T(8,128)S(1)} %get-tuple-element.5), kind=kLoop, calls=%fused_computation | loop fusion | flops 16384 | bytes 135168 | tf_op jit(solution)/shard_map/mul | solution.py:644

commit v5 on v4

--- a/solution.py
+++ b/solution.py
@@ -19,8 +19,9 @@
     for n in (1, 2, 3)
 )
 DIRECTIONS = FACES + EDGES + CORNERS
-FIELDS = 7
-SHALLOW, DEEP = 2, 4
+FIELDS = 9
+FIRST, DEEP = 3, 4
+MEMBRANE, SOURCE = 6, 7
 
 
 def tiles(reach):
@@ -303,59 +304,40 @@
     basis, coef, block, inverse,
     s_own, u_own, *refs,
 ):
-    groups = [refs[10 * n : 10 * n + 10] for n in range(4)]
-    gram_rows, gram_all, mine, parts, local_sem, sum_send, sum_recv = refs[40:]
+    groups = [refs[10 * n : 10 * n + 10] for n in range(3)]
+    gram_all, mine, parts, local_sem, sum_send, sum_recv = refs[30:]
     where = [lax.axis_index(a) for a in AXES]
-    cells, deep_cells, halo, deep_halo = (
+    s_deep = s_own.at[pl.ds(0, MEMBRANE + 1)]
+    cells, deep_cells, halo = (
         Halo(depth, (own, *group), where, sizes)
-        for depth, own, group in zip((SHALLOW, DEEP) * 2, (s_own, s_own, u_own, u_own), groups)
+        for depth, own, group in zip((FIRST, DEEP, DEEP), (s_own, s_deep, u_own), groups)
     )
 
-    every = slice(None)
-    near, rest, messages = [], [], []
-    for d in FACES:
-        if d[0]:
-            near.append(cells.planes(d, pl.ds(0, 2), 0, 1))
-            rest.append(cells.planes(d, pl.ds(2, 5), 0, 1))
-            rest.append(cells.planes(d, pl.ds(0, 2), 1, 1))
-        elif d[1]:
-            near.append(cells.rows(d, pl.ds(2, 2), 0, 1))
-            rest.append(cells.rows(d, pl.ds(0, 2), 0, 1))
-            rest.append(cells.rows(d, pl.ds(4, 3), 0, 1))
-            rest.append(cells.rows(d, pl.ds(2, 2), 1, 1))
-        else:
-            near.append(cells.columns(d))
-    for d in EDGES:
-        rest.append(cells.edge(d))
-
-    def all_messages(h, trim):
-        made = [h.edge(d) for d in (CORNERS if h.depth > 2 else []) + EDGES]
+    def all_messages(h, plane_sets):
+        made = [h.edge(d) for d in CORNERS + EDGES]
         for d in FACES:
-            if d[0] and trim:
-                made.append(h.planes(d, pl.ds(0, 2), 0, h.depth))
-                made.append(h.planes(d, pl.ds(2, 5), 0, h.depth - 1))
-            elif d[0]:
-                made.append(h.planes(d, every, 0, h.depth))
+            if d[0]:
+                made += [h.planes(d, fields, 0, count) for fields, count in plane_sets]
             elif d[1]:
-                made.append(h.rows(d, every, 0, h.depth))
+                made.append(h.rows(d, slice(None), 0, h.depth))
             else:
                 made.append(h.columns(d))
         return made
 
-    messages = all_messages(halo, False)
-    deep_rest = all_messages(deep_cells, True)
-    deep_messages = all_messages(deep_halo, False)
+    first_messages = all_messages(cells, [(pl.ds(0, 2), FIRST), (pl.ds(2, 7), FIRST - 1)])
+    deep_messages = all_messages(deep_cells, [(pl.ds(0, 2), DEEP), (pl.ds(2, 5), DEEP - 1)])
+    messages = all_messages(halo, [(slice(None), DEEP)])
 
     loads = [
         pltpu.make_async_copy(ref.at[axis], s_own.at[2 * axis + s], local_sem.at[2 * axis + s])
         for axis in range(3) for s, ref in enumerate((intra_hbm, extra_hbm))
     ] + [
         pltpu.make_async_copy(membrane_hbm, s_own.at[6], local_sem.at[6]),
-        pltpu.make_async_copy(source_hbm, basis.at[0], local_sem.at[7]),
+        pltpu.make_async_copy(source_hbm, s_own.at[pl.ds(7, 2)], local_sem.at[7]),
     ]
     for c in loads:
         c.start()
-    for h in (cells, deep_cells, halo, deep_halo):
+    for h in (cells, deep_cells, halo):
         for ref in (h.gx, h.gy, h.gz, h.gxy, h.gxz, h.gyz, h.gxyz):
             ref[...] = jnp.zeros_like(ref)
 
@@ -373,7 +355,7 @@
                 device_id_type=MESH,
             )
     for d in range(3):
-        for far in range(6, sizes[d]):
+        for far in range(5, sizes[d]):
             for step in (-far, far):
                 there = where[d] >= far if step < 0 else where[d] < sizes[d] - far
                 expected = expected + jnp.where(there, 1, 0)
@@ -391,11 +373,12 @@
     cells.fill_pack([s_own[f, x] for f in range(FIELDS) for x in range(NX)])
     pl.semaphore_wait(barrier, expected)
 
-    cells.start(0, near)
-    cells.start(0, rest)
-
-    def coefficients(view, beside, tiles):
-        for t in tiles:
+    cells.start(0, first_messages)
+    deep_cells.fill_pack([s_own[f, x] for f in range(MEMBRANE + 1) for x in range(NX)])
+    deep_cells.start(0, deep_messages)
+
+    def coefficients(view, cells_at):
+        for t in cells_at:
             n = PLACE[t]
             diagonals = []
             for s in range(2):
@@ -408,7 +391,7 @@
                     coef[s, n, 2 * axis + 1] = upper
                     total = upper + lower if total is None else total + upper + lower
                 diagonals.append(total)
-            di, de, m = diagonals[0], diagonals[1], view.tile(6, *t)
+            di, de, m = diagonals[0], diagonals[1], view.tile(MEMBRANE, *t)
             det = m * di + m * de + di * de
             inside = m > 0.0
             over = jnp.where(inside, 1.0 / jnp.where(inside, det, 1.0), 0.0)
@@ -418,14 +401,6 @@
             block[n, 3] = (m + di) * over
             if t in own:
                 inverse[t[0]] = (di + de) * over
-
-    def beside_own(view, f, t, axis, step):
-        if axis != 1:
-            return beside(view, f, t, axis, step)
-        row = NY - 1 if step < 0 else 0
-        edge = lax.broadcasted_iota(jnp.int32, TILE, 0) == NY - 1 - row
-        ghost = cells.gy[0, f, t[0], pl.ds(row, 1), :]
-        return jnp.where(edge, ghost, pltpu.roll(view.tile(f, *t), 1 if step < 0 else NY - 1, 0))
 
     own = [(x, OWN, OWN) for x in range(NX)]
     def solved(t, a, b):
@@ -462,82 +437,77 @@
         h.fill_pack(values[0] + values[1])
 
     def gram_row(k):
-        at = load(k)
-        for i in range(KRYLOV + 1):
+        at, first = load(k), k * (k + 1) // 2
+        for i in range(k + 1):
             total = None
             for s in range(2):
                 for x in range(NX):
                     term = at[s][x] * basis[i, s, x]
                     total = term if total is None else total + term
-            gram_rows[k, pl.ds(i, 1), :] = jnp.sum(total, axis=0, keepdims=True)
-
-    def powers(h, slot):
-        view, made = h.view(slot), []
-        for reach in range(h.depth - 1, -1, -1):
+            gram_all[pl.ds(first + i, 1), :] = jnp.sum(total, axis=0, keepdims=True)
+
+    def powers(view, depth):
+        made = []
+        for reach in range(depth - 1, -1, -1):
             now = {t: apply(view, t) for t in tiles(reach)}
             made.append([[now[t][s] for t in own] for s in range(2)])
             if reach:
-                then = {t: solved(t, *now[t]) for t in now}
-                view = Values([{t: then[t][s] for t in then} for s in range(2)])
+                view = solved_at(now)
         return made
+
+    def solved_at(pairs):
+        then = {t: solved(t, *pair) for t, pair in pairs.items()}
+        return Values([{t: then[t][s] for t in then} for s in range(2)])
 
     def combine(f, *vs):
         return [[f(*(v[s][x] for v in vs)) for x in range(NX)] for s in range(2)]
 
-    def advance(k, h, slot):
+    def advance(k, view, depth):
         here = load(k)
-        made = powers(h, slot)
+        made = powers(view, depth)
         terms = [
             made[0],
             combine(lambda b, a: 2.0 * b - a, made[1], here),
         ]
-        if h.depth > 2:
+        if depth > 2:
             terms.append(combine(lambda b, a: 4.0 * b - 3.0 * a, made[2], made[0]))
             terms.append(combine(lambda b, a, r: 8.0 * b - 8.0 * a + r, made[3], made[1], here))
         if k == 0:
             return terms
-        return [combine(lambda t, p: 2.0 * t - p, t, load(abs(k - 1 - j))) for j, t in enumerate(terms)]
-
-    cells.arrived(0, near)
-    coefficients(cells.view(0), beside_own, own)
-    stage(halo, load(0))
-    halo.start(0, messages)
-    deep_cells.fill_pack([s_own[f, x] for f in range(FIELDS) for x in range(NX)])
-    deep_cells.start(0, deep_rest)
-    gram_row(0)
-    cells.sent(0, near + rest)
-    cells.arrived(0, rest)
-    coefficients(cells.view(0), beside, [t for t in tiles(SHALLOW - 1) if t not in own])
-    halo.sent(0, messages)
-    halo.arrived(0, messages)
-    made = advance(0, halo, 0)
-    stage(deep_halo, made[-1])
-    deep_halo.start(0, deep_messages)
-    keep(1, made[0])
-    keep(2, made[1])
-    gram_row(1)
-    gram_row(2)
-    deep_cells.sent(0, deep_rest)
-    deep_cells.arrived(0, deep_rest)
-    coefficients(deep_cells.view(0), beside, [
-        t for t in TILES if t[1] == BESIDE or t[2] == BESIDE or t not in tiles(SHALLOW - 1)
-    ])
-    for slot, k in enumerate((2, 6)):
-        deep_halo.sent(slot, deep_messages)
-        deep_halo.arrived(slot, deep_messages)
-        made = advance(k, deep_halo, slot)
-        if slot == 0:
-            stage(deep_halo, made[-1])
-            deep_halo.start(1, deep_messages)
+        return [
+            combine(lambda t, p: 2.0 * t - p, t, load(abs(k - 1 - j))) for j, t in enumerate(terms)
+        ]
+
+    def extend(k, made):
         for j, v in enumerate(made):
             keep(k + 1 + j, v)
         for j in range(len(made)):
             gram_row(k + 1 + j)
 
-    at = 0
-    for k in range(KRYLOV + 1):
-        gram_all[pl.ds(at, k + 1), :] = gram_rows[k, pl.ds(0, k + 1), :]
-        at += k + 1
+    keep(0, [[s_own[SOURCE + s, x] for x in range(NX)] for s in range(2)])
+    gram_row(0)
+    cells.sent(0, first_messages)
+    cells.arrived(0, first_messages)
+    view = cells.view(0)
+    coefficients(view, tiles(FIRST - 1))
+    start = {t: [view.tile(SOURCE + s, *t) for s in range(2)] for t in tiles(FIRST - 1)}
+    made = advance(0, solved_at(start), FIRST - 1)
+    stage(halo, made[-1])
+    halo.start(0, messages)
+    extend(0, made)
+    deep_cells.sent(0, deep_messages)
+    deep_cells.arrived(0, deep_messages)
+    complete = [(x, OWN, OWN) for x in range(1 - FIRST, NX + FIRST - 1)]
+    coefficients(deep_cells.view(0), [t for t in TILES if t not in complete])
+    for slot, k in enumerate((2, 6)):
+        halo.sent(slot, messages)
+        halo.arrived(slot, messages)
+        made = advance(k, halo.view(slot), DEEP)
+        if slot == 0:
+            stage(halo, made[-1])
+            halo.start(1, messages)
+        extend(k, made)
+
     ones = jnp.ones(TILE, jnp.bfloat16)
     left, totals = gram_all[...], []
     for _ in range(3):
@@ -634,9 +604,9 @@
         scratch_shapes=[
             vm(KRYLOV + 1, 2, NX, *TILE), vm(2, count, 6, *TILE), vm(count, 4, *TILE), vm(NX, *TILE),
             vm(FIELDS, NX, *TILE), vm(2, NX, *TILE),
-            *halo_scratch(SHALLOW, FIELDS, 1, 28), *halo_scratch(DEEP, FIELDS, 1, 28),
-            *halo_scratch(SHALLOW, 2, 1, 18), *halo_scratch(DEEP, 2, 2, 26),
-            vm(KRYLOV + 1, 16, NZ), vm(128, NZ), vm(3, *TILE), vm(3, 8, *TILE),
+            *halo_scratch(FIRST, FIELDS, 1, 28), *halo_scratch(DEEP, MEMBRANE + 1, 1, 28),
+            *halo_scratch(DEEP, 2, 2, 26),
+            vm(128, NZ), vm(3, *TILE), vm(3, 8, *TILE),
             dma((8,)), dma((3, 8)), dma((3, 8)),
         ],
         compiler_params=pltpu.CompilerParams(collective_id=0, has_side_effects=True),

time: 49.1 us -> 47.9 us (0.976)
  Pallas kernels: 47.6 us -> 46.4 us
    pallas_call x1, Pallas kernels: 47.6 us -> 46.4 us  [body(): pl.pallas_call(functools.partial(cycle_kernel, sizes), out_shape=(vm(*sou...]
where the time goes in v5:
time: 47.9 us; the launch traced here: 47.7 us
  Pallas kernels  46.4 us (97%)
  between operations  0.64 us (1%)
  other arithmetic  0.63 us (1%)
    pallas_call x1, Pallas kernels, body(): pl.pallas_call(functools.partial(cycle_kernel, sizes), out_shape=(vm(*sou...  46.4 us

profile of v5, /device:TPU:1, one launch (start us, length us, event | category | flops | bytes accessed | tf_op | source)
XLA Modules:
  0.0 47.7 jit_solution(11743486731476498151)
XLA Ops:
  0.6 46.4 %shard_map.59 = (f32[2,4,8,128]{3,2,1,0:T(8,128)S(1)}, f32[2,4,8,128]{3,2,1,0:T(8,128)S(1)}, f32[8,128]{1,0:T(8,128)S(1)}) custom-call(f32[2,4,8,128]{3,2,1,0:T(8,128)} %source_hbm.1, f32[3,4,8,128]{3,2,1,0:T(8,128)} %intra_hbm.1, f32[3,4,8,128]{3,2,1,0:T(8,128)} %extra_hbm.1, f32[4,8,128]{2,1,0:T(8,128)} %membrane_hbm.1), custom_call_target="tpu_custom_call" | custom-call | tf_op jit(solution)/shard_map/pallas_call | solution.py:599
  47.1 0.6 %broadcast_multiply_fusion = (f32[2,4,8,128]{3,2,1,0:T(8,128)}, f32[2,4,8,128]{3,2,1,0:T(8,128)}) fusion(f32[2,4,8,128]{3,2,1,0:T(8,128)S(1)} %get-tuple-element.7, f32[8,128]{1,0:T(8,128)S(1)} %get-tuple-element.6, f32[2,4,8,128]{3,2,1,0:T(8,128)S(1)} %get-tuple-element.5), kind=kLoop, calls=%fused_computation | loop fusion | flops 16384 | bytes 135168 | tf_op jit(solution)/shard_map/mul | solution.py:614

commit v6 on v5

--- a/solution.py
+++ b/solution.py
@@ -76,7 +76,7 @@
 
     def planes(self, d, fields, first, count):
         low = NX - first - count if d[0] > 0 else first
-        at = self.depth - first - count if d[0] > 0 else first
+        at = DEEP - first - count if d[0] > 0 else first
         ghost = 0 if d[0] > 0 else 1
         return self.add(d, lambda slot: (
             self.own.at[fields, pl.ds(low, count)],
@@ -92,16 +92,20 @@
     def columns(self, d):
         return self.add(d, lambda slot: (self.pack, self.gz.at[slot, 0 if d[2] > 0 else 1]))
 
+    def corner_rows(self, d, fields, count):
+        planes = pl.ds(NX - count if d[0] > 0 else 0, count)
+        at = pl.ds(self.depth - 1 - count if d[0] > 0 else 0, count)
+        row = pl.ds(NY - count if d[1] > 0 else 0, count)
+        ghost = 0 if d[0] > 0 else 1
+        return self.add(d, lambda slot: (
+            self.own.at[fields, planes, row, :], self.gxy.at[slot, ghost, fields, at, row, :]
+        ))
+
     def edge(self, d):
         dx, dy, dz = d
         ghost_x, ghost_z = (0 if dx > 0 else 1), (0 if dz > 0 else 1)
         count = self.depth - sum(abs(a) for a in d) + 1
         row = pl.ds(NY - count if dy > 0 else 0, count)
-        if not dz:
-            planes = pl.ds(NX - count if dx > 0 else 0, count)
-            return self.add(d, lambda slot: (
-                self.own.at[:, planes, row, :], self.gxy.at[slot, ghost_x, :, :, row, :]
-            ))
         if not dy:
             return self.add(d, lambda slot: (self.pack, self.gxz.at[slot, ghost_x, ghost_z]))
         if not dx:
@@ -179,7 +183,7 @@
             return h.gxy[self.slot, outside[0], f, x + h.depth - 1 if x < 0 else x - NX]
         if not outside:
             return h.own[f, x]
-        return h.gx[self.slot, outside[0], f, x + h.depth if x < 0 else x - NX]
+        return h.gx[self.slot, outside[0], f, x + DEEP if x < 0 else x - NX]
 
 
 class Values:
@@ -313,20 +317,31 @@
         for depth, own, group in zip((FIRST, DEEP, DEEP), (s_own, s_deep, u_own), groups)
     )
 
-    def all_messages(h, plane_sets):
-        made = [h.edge(d) for d in CORNERS + EDGES]
+    deep_cells.gx = cells.gx
+
+    def all_messages(h, plane_sets, row_sets):
+        made = [h.edge(d) for d in CORNERS]
+        for d in EDGES:
+            if d[2]:
+                made.append(h.edge(d))
+            else:
+                made += [h.corner_rows(d, *fields) for fields in row_sets]
         for d in FACES:
             if d[0]:
-                made += [h.planes(d, fields, 0, count) for fields, count in plane_sets]
+                made += [h.planes(d, *planes) for planes in plane_sets]
             elif d[1]:
                 made.append(h.rows(d, slice(None), 0, h.depth))
             else:
                 made.append(h.columns(d))
         return made
 
-    first_messages = all_messages(cells, [(pl.ds(0, 2), FIRST), (pl.ds(2, 7), FIRST - 1)])
-    deep_messages = all_messages(deep_cells, [(pl.ds(0, 2), DEEP), (pl.ds(2, 5), DEEP - 1)])
-    messages = all_messages(halo, [(slice(None), DEEP)])
+    first_messages = all_messages(cells, [
+        (pl.ds(0, 2), 0, FIRST), (pl.ds(2, 7), 0, FIRST - 1),
+    ], [(pl.ds(0, 4), FIRST - 1), (pl.ds(4, 5), FIRST - 2)])
+    deep_messages = all_messages(deep_cells, [
+        (pl.ds(0, 2), FIRST, 1), (pl.ds(2, 5), FIRST - 1, 1),
+    ], [(pl.ds(0, 4), DEEP - 1), (pl.ds(4, 3), DEEP - 2)])
+    messages = all_messages(halo, [(slice(None), 0, DEEP)], [(slice(None), DEEP - 1)])
 
     loads = [
         pltpu.make_async_copy(ref.at[axis], s_own.at[2 * axis + s], local_sem.at[2 * axis + s])
@@ -583,7 +598,7 @@
     packs = -(-fields * NX // (NZ // (2 * depth)))
     return [
         vm(packs, *TILE),
-        vm(slots, 2, fields, depth, *TILE), vm(slots, fields, NX, *TILE),
+        vm(slots, 2, fields, DEEP, *TILE), vm(slots, fields, NX, *TILE),
         vm(slots, 2, packs, *TILE), vm(slots, 2, fields, depth - 1, *TILE),
         vm(slots, 2, 2, packs, *TILE), vm(slots, 2, packs, *TILE), vm(slots, 2, 2, packs, *TILE),
         dma((count,)), dma((slots, count)),
@@ -604,7 +619,7 @@
         scratch_shapes=[
             vm(KRYLOV + 1, 2, NX, *TILE), vm(2, count, 6, *TILE), vm(count, 4, *TILE), vm(NX, *TILE),
             vm(FIELDS, NX, *TILE), vm(2, NX, *TILE),
-            *halo_scratch(FIRST, FIELDS, 1, 28), *halo_scratch(DEEP, MEMBRANE + 1, 1, 28),
+            *halo_scratch(FIRST, FIELDS, 1, 32), *halo_scratch(DEEP, MEMBRANE + 1, 1, 32),
             *halo_scratch(DEEP, 2, 2, 26),
             vm(128, NZ), vm(3, *TILE), vm(3, 8, *TILE),
             dma((8,)), dma((3, 8)), dma((3, 8)),

time: 47.9 us -> 47.4 us (0.990)
  Pallas kernels: 46.4 us -> 45.6 us
    pallas_call x1, Pallas kernels: 46.4 us -> 45.6 us  [body(): pl.pallas_call(functools.partial(cycle_kernel, sizes), out_shape=(vm(*sou...]
where the time goes in v6:
time: 47.4 us; the launch traced here: 46.8 us
  Pallas kernels  45.6 us (96%)
  between operations  0.64 us (1%)
  other arithmetic  0.63 us (1%)
    pallas_call x1, Pallas kernels, body(): pl.pallas_call(functools.partial(cycle_kernel, sizes), out_shape=(vm(*sou...  45.6 us

profile of v6, /device:TPU:1, one launch (start us, length us, event | category | flops | bytes accessed | tf_op | source)
XLA Modules:
  0.0 46.8 jit_solution(5507788590992080908)
XLA Ops:
  0.6 45.6 %shard_map.59 = (f32[2,4,8,128]{3,2,1,0:T(8,128)S(1)}, f32[2,4,8,128]{3,2,1,0:T(8,128)S(1)}, f32[8,128]{1,0:T(8,128)S(1)}) custom-call(f32[2,4,8,128]{3,2,1,0:T(8,128)} %source_hbm.1, f32[3,4,8,128]{3,2,1,0:T(8,128)} %intra_hbm.1, f32[3,4,8,128]{3,2,1,0:T(8,128)} %extra_hbm.1, f32[4,8,128]{2,1,0:T(8,128)} %membrane_hbm.1), custom_call_target="tpu_custom_call" | custom-call | tf_op jit(solution)/shard_map/pallas_call | solution.py:614
  46.2 0.6 %broadcast_multiply_fusion = (f32[2,4,8,128]{3,2,1,0:T(8,128)}, f32[2,4,8,128]{3,2,1,0:T(8,128)}) fusion(f32[2,4,8,128]{3,2,1,0:T(8,128)S(1)} %get-tuple-element.7, f32[8,128]{1,0:T(8,128)S(1)} %get-tuple-element.6, f32[2,4,8,128]{3,2,1,0:T(8,128)S(1)} %get-tuple-element.5), kind=kLoop, calls=%fused_computation | loop fusion | flops 16384 | bytes 135168 | tf_op jit(solution)/shard_map/mul | solution.py:629

commit v7 on v6

--- a/solution.py
+++ b/solution.py
@@ -352,9 +352,13 @@
     ]
     for c in loads:
         c.start()
-    for h in (cells, deep_cells, halo):
+    def clear(h):
         for ref in (h.gx, h.gy, h.gz, h.gxy, h.gxz, h.gyz, h.gxyz):
-            ref[...] = jnp.zeros_like(ref)
+            if h is not deep_cells or ref is not h.gx:
+                ref[...] = jnp.zeros_like(ref)
+
+    clear(cells)
+    clear(deep_cells)
 
     barrier = pltpu.get_barrier_semaphore()
     expected = 0
@@ -381,6 +385,7 @@
                         barrier, inc=1, device_id={AXES[d]: lax.rem(where[d] + step + sizes[d], sizes[d])}, device_id_type=MESH
                     )
     gram_all[...] = jnp.zeros_like(gram_all)
+    clear(halo)
     for k in range(1, KRYLOV + 1):
         basis[k] = jnp.zeros_like(basis.at[k])
     for c in loads:

time: 47.4 us -> 47.3 us (level)
  no operation moved by 1% of the time
where the time goes in v7:
time: 47.3 us; the launch traced here: 46.8 us
  Pallas kernels  45.6 us (96%)
  between operations  0.64 us (1%)
  other arithmetic  0.63 us (1%)
    pallas_call x1, Pallas kernels, body(): pl.pallas_call(functools.partial(cycle_kernel, sizes), out_shape=(vm(*sou...  45.6 us

profile of v7, /device:TPU:1, one launch (start us, length us, event | category | flops | bytes accessed | tf_op | source)
XLA Modules:
  0.0 46.8 jit_solution(10051293278697911226)
XLA Ops:
  0.6 45.6 %shard_map.59 = (f32[2,4,8,128]{3,2,1,0:T(8,128)S(1)}, f32[2,4,8,128]{3,2,1,0:T(8,128)S(1)}, f32[8,128]{1,0:T(8,128)S(1)}) custom-call(f32[2,4,8,128]{3,2,1,0:T(8,128)} %source_hbm.1, f32[3,4,8,128]{3,2,1,0:T(8,128)} %intra_hbm.1, f32[3,4,8,128]{3,2,1,0:T(8,128)} %extra_hbm.1, f32[4,8,128]{2,1,0:T(8,128)} %membrane_hbm.1), custom_call_target="tpu_custom_call" | custom-call | tf_op jit(solution)/shard_map/pallas_call | solution.py:619
  46.2 0.6 %broadcast_multiply_fusion = (f32[2,4,8,128]{3,2,1,0:T(8,128)}, f32[2,4,8,128]{3,2,1,0:T(8,128)}) fusion(f32[2,4,8,128]{3,2,1,0:T(8,128)S(1)} %get-tuple-element.7, f32[8,128]{1,0:T(8,128)S(1)} %get-tuple-element.6, f32[2,4,8,128]{3,2,1,0:T(8,128)S(1)} %get-tuple-element.5), kind=kLoop, calls=%fused_computation | loop fusion | flops 16384 | bytes 135168 | tf_op jit(solution)/shard_map/mul | solution.py:634
